TPU v7x, 32 devices: a whole 2x2x4 slice. The times are simulated.
32 devices in a mesh: gz: 8 (over y, x, core), gy: 4 (over z).
Axes of the slice: x: 2, y: 2, z: 4, core: 2. Of those that a mesh axis runs over, the one named last changes fastest.
Arguments:
- source: float32 [128, 256, 256], P(('gz', 'gy')), may hold values from -8 to 8
- vertical: float32 [128], P(('gz', 'gy')), may hold values from 1 to 64
- reaction: float32 [128, 256, 256], P(('gz', 'gy')), may hold values from 0.05 to 2
Outputs:
- solution: float32 [128, 256, 256], P(('gz', 'gy'))
- norms: float32 [2], replicated
All inputs are finite; a program needn't handle non-finite values.
Results may differ from a plain program's by a relative error of at most 0.0001.
Values sent between devices are 32-bit elements; how exact they have to be, the bound alone decides.
A program may use at most 192 MiB of HBM per device.

v0:
```python
import functools

import jax
import jax.numpy as jnp
import numpy as np
from jax import lax
from jax.experimental import pallas as pl
from jax.experimental.pallas import tpu as pltpu
from jax.sharding import PartitionSpec as P

LEVELS = 5
SWITCH = 2
CYCLES = 2
SWEEPS = 2
COARSE = 4
DAMPING = 0.8
COUPLING = 1.0
CHUNK = 32
MESH = pl.DeviceIdType.MESH


def dot(a, b):
    return lax.dot_general(
        a,
        b,
        (((1,), (0,)), ((), ())),
        precision=lax.Precision.HIGHEST,
        preferred_element_type=jnp.float32,
    )


def parts_of(x):
    first = x.astype(jnp.bfloat16)
    rest = x - first.astype(jnp.float32)
    second = rest.astype(jnp.bfloat16)
    third = (rest - second.astype(jnp.float32)).astype(jnp.bfloat16)
    return (third, second, first)


def dot_right(x, m):
    m = m.astype(jnp.bfloat16)
    total = None
    for x in parts_of(x):
        term = jnp.dot(x, m, preferred_element_type=jnp.float32)
        total = term if total is None else total + term
    return total


def dot_left(m, x):
    m = m.astype(jnp.bfloat16)
    total = None
    for x in parts_of(x):
        term = jnp.dot(m, x, preferred_element_type=jnp.float32)
        total = term if total is None else total + term
    return total


def kernel(
    dims,
    source, reaction, vert_s, vert_b, down0, downt0, down1, cols, mask, group, ups, groupt, colst,
    out, norms,
    v0, v1, w0, d1, w1, g1, r1, tmp0, res1, corr1, send_a, recv_a, send_v, recv_v, recv_b,
    send_n, recv_n, lines, diag, factor, target, around, halo, rowbuf, acc,
    plane_send, plane_recv, line_send, line_recv, a2a_send, a2a_recv,
):
    gz, gy, depth, cp = dims
    nd = gz * gy
    zall = nd * depth
    n0 = source.shape[1]
    n1 = n0 // 2
    a_me = lax.axis_index("gz")
    b_me = lax.axis_index("gy")
    me = a_me * gy + b_me
    h = [COUPLING / 4.0**k for k in range(LEVELS)]

    @pl.when(me == 0)
    def _():
        for p in range(2):
            v0[p, 0] = jnp.zeros((n0, n0), jnp.float32)
            v1[p, 0] = jnp.zeros((n1, n1), jnp.float32)

    @pl.when(me == nd - 1)
    def _():
        for p in range(2):
            v0[p, depth + 1] = jnp.zeros((n0, n0), jnp.float32)
            v1[p, depth + 1] = jnp.zeros((n1, n1), jnp.float32)

    edges = [a_me == 0, a_me == gz - 1, b_me == 0, b_me == gy - 1]
    for k in range(4):
        @pl.when(edges[k])
        def _(k=k):
            for p in range(2):
                halo[p, k] = jnp.zeros((zall, cp), jnp.float32)

    def flat(d):
        return (d // gy, d % gy)

    def plane_copy(v, p, level, up):
        if up:
            src, dst, to = v.at[p, depth], v.at[p, 0], flat(me + 1)
        else:
            src, dst, to = v.at[p, 1], v.at[p, depth + 1], flat(me + nd - 1 - nd * ((me + nd - 1) // nd))
        if up:
            to = flat((me + 1) % nd)
        k = 0 if up else 1
        return pltpu.make_async_remote_copy(
            src_ref=src, dst_ref=dst,
            send_sem=plane_send.at[level, p, k], recv_sem=plane_recv.at[level, p, k],
            device_id=to, device_id_type=MESH,
        )

    def plane_start(v, p, level):
        @pl.when(me < nd - 1)
        def _():
            plane_copy(v, p, level, True).start()

        @pl.when(me > 0)
        def _():
            plane_copy(v, p, level, False).start()

    def plane_wait(v, p, level):
        @pl.when(me < nd - 1)
        def _():
            plane_copy(v, p, level, True).wait_send()
            plane_copy(v, p, level, False).wait_recv()

        @pl.when(me > 0)
        def _():
            plane_copy(v, p, level, False).wait_send()
            plane_copy(v, p, level, True).wait_recv()

    def residual_chunk(v, p, z, r, n, target_ref, diag_of, weight):
        centre = v[p, z, pl.ds(r, CHUNK), :]
        rows = lax.broadcasted_iota(jnp.int32, (CHUNK, n), 0)
        lanes = lax.broadcasted_iota(jnp.int32, (CHUNK, n), 1)
        if r == 0:
            above = jnp.where(rows == 0, 0.0, pltpu.roll(centre, 1, 0))
        else:
            above = v[p, z, pl.ds(r - 1, CHUNK), :]
        if r + CHUNK == n:
            below = jnp.where(rows == CHUNK - 1, 0.0, pltpu.roll(centre, CHUNK - 1, 0))
        else:
            below = v[p, z, pl.ds(r + 1, CHUNK), :]
        left = jnp.where(lanes == 0, 0.0, pltpu.roll(centre, 1, 1))
        right = jnp.where(lanes == n - 1, 0.0, pltpu.roll(centre, n - 1, 1))
        vert = vert_s[z - 1]
        applied = (
            diag_of(z - 1, r, vert) * centre
            - vert * (v[p, z - 1, pl.ds(r, CHUNK), :] + v[p, z + 1, pl.ds(r, CHUNK), :])
            - weight * (above + below + left + right)
        )
        return centre, target_ref[z - 1, pl.ds(r, CHUNK), :] - applied

    def diag0(z, r, vert):
        return 2.0 * vert + 4.0 * h[0] + reaction[z, pl.ds(r, CHUNK), :]

    def diag1(z, r, vert):
        return d1[z, pl.ds(r, CHUNK), :]

    def over_planes(v, p, level, body):
        plane_start(v, p, level)

        def inner(z, c):
            body(z)
            return c

        lax.fori_loop(2, depth, inner, 0)
        plane_wait(v, p, level)

        def outer(i, c):
            body(1 + i * (depth - 1))
            return c

        lax.fori_loop(0, 2, outer, 0)

    def level_parts(level):
        if level == 0:
            return v0, source, diag0, w0, n0
        return v1, g1, diag1, w1, n1

    def sweep(level, p, record=None):
        v, tgt, dg, w, n = level_parts(level)

        def body(z):
            for r in range(0, n, CHUNK):
                centre, res = residual_chunk(v, p, z, r, n, tgt, dg, h[level])
                v[1 - p, z, pl.ds(r, CHUNK), :] = centre + w[z - 1, pl.ds(r, CHUNK), :] * res
                if record is not None:
                    sq = (res * res).reshape(CHUNK // 8, 8, n).sum(axis=0)
                    acc[record, :, :] += sq

        over_planes(v, p, level, body)
        return 1 - p

    def first_sweep(level):
        v, tgt, dg, w, n = level_parts(level)

        def body(z, c):
            v[0, z + 1] = w[z] * tgt[z]
            return c

        lax.fori_loop(0, depth, body, 0)
        return 0

    def restrict0(read_chunk, store):
        def body(z):
            for r in range(0, n0, CHUNK):
                tmp0[pl.ds(r, CHUNK), :] = dot_right(read_chunk(z, r), downt0[...])
            store(z, dot_left(down0[...], tmp0[...]))
        return body

    def restrict1(z, plane):
        half = dot(down1[...], plane)
        for b in range(gy):
            spread = dot(half, cols[b]) * mask[...]
            packed = dot(group[...], spread)
            for a in range(gz):
                send_a[b, a, z : z + 1, :] = packed[a : a + 1, :]

    def exchange_all(kind, src_of, recv):
        def copy(k):
            dst = (me + k) % nd
            a, b = dst // gy, dst % gy
            return pltpu.make_async_remote_copy(
                src_ref=src_of(a, b), dst_ref=recv.at[b_me, a_me],
                send_sem=a2a_send.at[kind, k], recv_sem=a2a_recv.at[kind, me],
                device_id=(a, b), device_id_type=MESH,
            )

        def start(k, c):
            copy(k).start()
            return c

        def finish(k, c):
            copy(k).wait_send()
            src = (me + k) % nd
            a, b = src // gy, src % gy
            pltpu.make_async_remote_copy(
                src_ref=recv.at[b, a], dst_ref=recv.at[b, a],
                send_sem=a2a_send.at[kind, k], recv_sem=a2a_recv.at[kind, src],
                device_id=(a, b), device_id_type=MESH,
            ).wait_recv()
            return c

        def begin():
            lax.fori_loop(1, nd, start, 0)

        def end():
            lax.fori_loop(1, nd, finish, 0)

        return begin, end

    def to_lines(recv, dest):
        for a in range(gz):
            for b in range(gy):
                s = (a * gy + b) * depth
                dest[s : s + depth, :] = recv[b, a]

    bx2, by2 = (n1 // 2 // gz, n1 // 2 // gy)
    steps = []
    s = 1
    while s < zall:
        steps.append(s)
        s *= 2
    ns = len(steps)

    def setup_lines(offset):
        rows = lax.broadcasted_iota(jnp.int32, (zall, cp), 0)
        vert = lines[...]
        a = jnp.where(rows == 0, 0.0, -vert)
        c = jnp.where(rows == zall - 1, 0.0, -vert)
        b = diag[offset]
        for k, s in enumerate(steps):
            alpha = -a / pltpu.roll(b, s, 0)
            gamma = -c / pltpu.roll(b, zall - s, 0)
            b = b + alpha * pltpu.roll(c, s, 0) + gamma * pltpu.roll(a, zall - s, 0)
            a = alpha * pltpu.roll(a, s, 0)
            c = gamma * pltpu.roll(c, zall - s, 0)
            factor[offset, 2 * k] = alpha
            factor[offset, 2 * k + 1] = gamma
        factor[offset, 2 * ns] = 1.0 / b

    def solve(offset, right):
        for k, s in enumerate(steps):
            right = (
                right
                + factor[offset, 2 * k] * pltpu.roll(right, s, 0)
                + factor[offset, 2 * k + 1] * pltpu.roll(right, zall - s, 0)
            )
        return right * factor[offset, 2 * ns]

    count = [0]
    def line_copy(p, k):
        if k == 0:
            to, slot = ((a_me + gz - 1) % gz, b_me), 1
        elif k == 1:
            to, slot = ((a_me + 1) % gz, b_me), 0
        elif k == 2:
            to, slot = (a_me, (b_me + gy - 1) % gy), 3
        else:
            to, slot = (a_me, (b_me + 1) % gy), 2
        return pltpu.make_async_remote_copy(
            src_ref=around.at[p], dst_ref=halo.at[p, slot],
            send_sem=line_send.at[p, k], recv_sem=line_recv.at[p, slot],
            device_id=to, device_id_type=MESH,
        )

    def line_landed(p, k):
        return pltpu.make_async_remote_copy(
            src_ref=around.at[p], dst_ref=halo.at[p, k],
            send_sem=line_send.at[p, k], recv_sem=line_recv.at[p, k],
            device_id=(a_me, b_me), device_id_type=MESH,
        )

    def neighbours(offset, values):
        bx, by = bx2 >> offset, by2 >> offset
        cells = bx * by
        p = count[0] % 2
        count[0] += 1
        around[p] = values
        for k in range(4):
            @pl.when(jnp.logical_not(edges[k]))
            def _(k=k):
                line_copy(p, k).start()
        for k in range(4):
            @pl.when(jnp.logical_not(edges[k]))
            def _(k=k):
                line_copy(p, k).wait_send()
                line_landed(p, k).wait_recv()
        lane = lax.broadcasted_iota(jnp.int32, (zall, cp), 1)

        def roll(x, amount):
            amount = amount % cp
            return x if amount == 0 else pltpu.roll(x, amount, 1)

        total = jnp.where(lane < by, roll(halo[p, 0], by - cells), roll(values, by))
        total += jnp.where(lane >= cells - by, roll(halo[p, 1], cells - by), roll(values, -by))
        inrow = lane & (by - 1)
        total += jnp.where(inrow == 0, roll(halo[p, 2], 1 - by), roll(values, 1))
        total += jnp.where(inrow == by - 1, roll(halo[p, 3], by - 1), roll(values, -1))
        return total

    def line_descend(offset):
        weight = h[SWITCH + offset]
        values = solve(offset, target[offset])
        repeats = COARSE if offset == LEVELS - 1 - SWITCH else SWEEPS
        for _ in range(1, repeats):
            values = solve(offset, target[offset] + weight * neighbours(offset, values))
        if offset == LEVELS - 1 - SWITCH:
            return values
        near = neighbours(offset, values)
        rows = lax.broadcasted_iota(jnp.int32, (zall, cp), 0)
        before = jnp.where(rows == 0, 0.0, pltpu.roll(values, 1, 0))
        after = jnp.where(rows == zall - 1, 0.0, pltpu.roll(values, zall - 1, 0))
        res = target[offset] - (
            diag[offset] * values - lines[...] * (before + after) - weight * near
        )
        target[offset + 1] = dot(res, ups[2 * offset])
        tmp = values
        lower = line_descend(offset + 1)
        values = tmp + dot(lower, ups[2 * offset + 1])
        for _ in range(SWEEPS):
            values = solve(offset, target[offset] + weight * neighbours(offset, values))
        return values

    def fill0(z, c):
        w0[z] = DAMPING / (2.0 * vert_s[z] + 4.0 * h[0] + reaction[z])
        return c

    lax.fori_loop(0, depth, fill0, 0)

    def keep_r1(z, value):
        r1[z] = value
        dv = 2.0 * vert_s[z] + 4.0 * h[1] + value
        d1[z] = dv
        w1[z] = DAMPING / dv

    body = restrict0(lambda z, r: reaction[z, pl.ds(r, CHUNK), :], keep_r1)
    lax.fori_loop(0, depth, lambda z, c: (body(z), c)[1], 0)
    for z in range(depth):
        restrict1(z, r1[z])
    send_v[...] = send_a[...]
    begin_v, end_v = exchange_all(0, lambda a, b: vert_b, recv_v)
    begin_r, end_r = exchange_all(1, lambda a, b: send_v.at[b, a], recv_a)
    begin_v()
    begin_r()
    recv_v[b_me, a_me] = vert_b[...]
    recv_a[b_me, a_me] = send_v[b_me, a_me]
    acc[...] = jnp.zeros_like(acc)

    begin_a, end_a = exchange_all(2, lambda a, b: send_a.at[b, a], recv_b.at[0])
    begin_b, end_b = exchange_all(3, lambda a, b: send_n.at[b, a], recv_b.at[1])

    p0 = first_sweep(0)
    for cycle in range(CYCLES):
        for k in range(SWEEPS):
            if cycle == 0 and k == 0:
                continue
            p0 = sweep(0, p0, record=cycle - 1 if cycle > 0 and k == 0 else None)

        def read0(z, r, p0=p0):
            return residual_chunk(v0, p0, z, r, n0, source, diag0, h[0])[1]

        def keep_g1(z, value):
            g1[z - 1] = value

        over_planes(v0, p0, 0, restrict0(read0, keep_g1))
        p1 = first_sweep(1)
        for k in range(1, SWEEPS):
            p1 = sweep(1, p1)

        def keep_res(z, p1=p1):
            for r in range(0, n1, CHUNK):
                res1[z - 1, pl.ds(r, CHUNK), :] = residual_chunk(
                    v1, p1, z, r, n1, g1, diag1, h[1]
                )[1]

        over_planes(v1, p1, 1, keep_res)
        for z in range(depth):
            restrict1(z, res1[z])
        begin_a()
        recv_b[0, b_me, a_me] = send_a[b_me, a_me]
        if cycle == 0:
            end_v()
            end_r()
            to_lines(recv_v, lines)
            to_lines(recv_a, target.at[0])
            coarse = target[0]
            for offset in range(LEVELS - SWITCH):
                if offset > 0:
                    coarse = dot(coarse, ups[2 * offset - 2])
                diag[offset] = 2.0 * lines[...] + 4.0 * h[SWITCH + offset] + coarse
            for offset in range(LEVELS - SWITCH):
                setup_lines(offset)
        end_a()
        to_lines(recv_b.at[0], target.at[0])
        rowbuf[...] = line_descend(0)
        for a in range(gz):
            for b in range(gy):
                s = (a * gy + b) * depth
                send_n[b, a] = rowbuf[s : s + depth, :]
        begin_b()
        recv_b[1, b_me, a_me] = send_n[b_me, a_me]
        end_b()
        for z in range(depth):
            wide = None
            for b in range(gy):
                for a in range(gz):
                    corr1[a : a + 1, :] = recv_b[1, b, a, z : z + 1, :]
                part = dot(dot(groupt[...], corr1[...]) * mask[...], colst[b])
                wide = part if wide is None else wide + part
            v1[1 - p1, z + 1] = v1[p1, z + 1] + dot(down1[...].T * 2.0, wide)
        p1 = 1 - p1
        for _ in range(SWEEPS):
            p1 = sweep(1, p1)

        def correct0(z, c, p0=p0, p1=p1):
            tmp0[...] = dot_left(downt0[...] * 2.0, v1[p1, z])
            for r in range(0, n0, CHUNK):
                v0[1 - p0, z, pl.ds(r, CHUNK), :] = v0[p0, z, pl.ds(r, CHUNK), :] + dot_right(
                    tmp0[pl.ds(r, CHUNK), :], down0[...] * 2.0
                )
            return c

        lax.fori_loop(1, depth + 1, correct0, 0)
        p0 = 1 - p0
        for _ in range(SWEEPS):
            p0 = sweep(0, p0)

    def last(z, p0=p0):
        for r in range(0, n0, CHUNK):
            centre, res = residual_chunk(v0, p0, z, r, n0, source, diag0, h[0])
            out[z - 1, pl.ds(r, CHUNK), :] = centre
            acc[CYCLES - 1, :, :] += (res * res).reshape(CHUNK // 8, 8, n0).sum(axis=0)

    over_planes(v0, p0, 0, last)
    ridx = lax.broadcasted_iota(jnp.int32, (8, 128), 0)
    part = jnp.zeros((8, 128), jnp.float32)
    for k in range(CYCLES):
        part = jnp.where(ridx == k, jnp.sum(acc[k]), part)
    rowbuf_n = tmp_n = send_n
    target_n = recv_n
    w_n = acc
    acc[0, :, 0:128] = part
    begin_n, end_n = exchange_all(4, lambda a, b: acc.at[0, :, pl.ds(0, 128)], recv_n)
    begin_n()
    recv_n[b_me, a_me] = part
    end_n()
    total = jnp.zeros((8, 128), jnp.float32)
    for a in range(gz):
        for b in range(gy):
            total = total + recv_n[b, a]
    norms[...] = total * (1.0 / (zall * n0 * n0))


def pair_matrix(n, value):
    return (np.arange(n)[None, :] // 2 == np.arange(n // 2)[:, None]).astype(np.float32) * value


def shards(gz, gy, source, vertical, reaction):
    depth, n0 = source.shape[0], source.shape[1]
    nd = gz * gy
    zall = nd * depth
    n1, n2 = n0 // 2, n0 // 4
    bx, by = n2 // gz, n2 // gy
    cells = bx * by
    cp = -(-cells // 128) * 128
    down0 = pair_matrix(n0, 0.5)
    down1 = pair_matrix(n1, 0.5)
    lane = np.arange(cp)
    cols = np.zeros((gy, n1, cp), np.float32)
    colst = np.zeros((gy, cp, n1), np.float32)
    for b in range(gy):
        hit = (np.arange(n1)[:, None] // 2 == b * by + lane[None, :] % by) & (lane[None, :] < cells)
        cols[b] = hit * 0.5
        colst[b] = hit.T
    mask = ((lane[None, :] // by == np.arange(n2)[:, None] % bx) & (lane[None, :] < cells)).astype(np.float32)
    group = (np.arange(n2)[None, :] // bx == np.arange(gz)[:, None]).astype(np.float32)
    ups = []
    for offset in range(LEVELS - SWITCH - 1):
        fx, fy = bx >> offset, by >> offset
        cy = fy // 2
        matrix = np.zeros((cp, cp), np.float32)
        for i in range(fx):
            for j in range(fy):
                matrix[i * fy + j, (i // 2) * cy + j // 2] = 1.0
        ups += [matrix * 0.25, matrix.T]
    ups = np.stack(ups)
    steps = (zall - 1).bit_length()
    f32 = jnp.float32
    nl = LEVELS - SWITCH
    vm = pl.BlockSpec(memory_space=pltpu.VMEM)
    consts = [down0, down0.T.copy(), down1, cols, mask, group, ups, group.T.copy(), colst]
    solution, norms = pl.pallas_call(
        functools.partial(kernel, (gz, gy, depth, cp)),
        out_shape=(
            jax.ShapeDtypeStruct(source.shape, f32),
            jax.ShapeDtypeStruct((8, 128), f32),
        ),
        in_specs=[vm, vm, pl.BlockSpec(memory_space=pltpu.SMEM), vm] + [vm] * len(consts),
        out_specs=(vm, vm),
        scratch_shapes=[
            pltpu.VMEM((2, depth + 2, n0, n0), f32),
            pltpu.VMEM((2, depth + 2, n1, n1), f32),
            pltpu.VMEM((depth, n0, n0), f32),
            pltpu.VMEM((depth, n1, n1), f32),
            pltpu.VMEM((depth, n1, n1), f32),
            pltpu.VMEM((depth, n1, n1), f32),
            pltpu.VMEM((depth, n1, n1), f32),
            pltpu.VMEM((n0, n1), f32),
            pltpu.VMEM((depth, n1, n1), f32),
            pltpu.VMEM((gz, cp), f32),
            pltpu.VMEM((gy, gz, depth, cp), f32),
            pltpu.VMEM((gy, gz, depth, cp), f32),
            pltpu.VMEM((gy, gz, depth, cp), f32),
            pltpu.VMEM((gy, gz, depth, cp), f32),
            pltpu.VMEM((2, gy, gz, depth, cp), f32),
            pltpu.VMEM((gy, gz, depth, cp), f32),
            pltpu.VMEM((gy, gz, 8, 128), f32),
            pltpu.VMEM((zall, cp), f32),
            pltpu.VMEM((nl, zall, cp), f32),
            pltpu.VMEM((nl, 2 * steps + 1, zall, cp), f32),
            pltpu.VMEM((nl, zall, cp), f32),
            pltpu.VMEM((2, zall, cp), f32),
            pltpu.VMEM((2, 4, zall, cp), f32),
            pltpu.VMEM((zall, cp), f32),
            pltpu.VMEM((CYCLES, 8, n0), f32),
            pltpu.SemaphoreType.DMA((2, 2, 2)),
            pltpu.SemaphoreType.DMA((2, 2, 2)),
            pltpu.SemaphoreType.DMA((2, 4)),
            pltpu.SemaphoreType.DMA((2, 4)),
            pltpu.SemaphoreType.DMA((5, nd)),
            pltpu.SemaphoreType.DMA((5, nd)),
        ],
        compiler_params=pltpu.CompilerParams(
            has_side_effects=True, vmem_limit_bytes=64000 * 1024
        ),
    )(
        source,
        reaction,
        vertical,
        jnp.broadcast_to(vertical[:, None], (depth, cp)),
        *[jnp.asarray(c) for c in consts],
    )
    return solution, norms[:CYCLES, 0]


def solution(mesh):
    return jax.shard_map(
        functools.partial(shards, mesh.shape["gz"], mesh.shape["gy"]),
        mesh=mesh,
        in_specs=(P(("gz", "gy"), None, None), P(("gz", "gy")), P(("gz", "gy"), None, None)),
        out_specs=(P(("gz", "gy"), None, None), P()),
        check_vma=False,
    )
```

profile of v0, /device:TPU:0, one launch (start us, length us, event | category | flops | bytes accessed | tf_op | source)
XLA Modules:
  0.0 342.2 jit_solution(14245980939128280456)
XLA Ops:
  0.6 1.3 broadcast_in_dim.2.vert_b
  1.9 336.7 %shard_map.131 = (f32[4,256,256]{2,1,0:T(8,128)}, f32[8,128]{1,0:T(8,128)}) custom-call(f32[4,256,256]{2,1,0:T(8,128)} %source.1, f32[4,256,256]{2,1,0:T(8,128)} %reaction.1, f32[4]{0:T(128)} %vert_s.1, f32[4,128]{1,0:T(4,128)} %broadcast_in_dim.2.vert_b, f32[128,256]{1,0:T(8,128)} %constant.18.clone.down0, f32[256,128]{1,0:T(8,128)} %constant.19.clone.downt0, ...), custom_call_target="tpu_custom_call" | custom-call | tf_op jit(solution)/shard_map/pallas_call | solution.py:534
  338.6 1.3 slice_reduce_fusion
  339.9 2.3 copy.15
where the time goes:
time: 342 us
  Pallas kernels  337 us (99%)
  local copies, waits for them, and re-layouts  4.89 us (1%)
    pallas_call x1, Pallas kernels, shards(): pl.pallas_call(functools.partial(kernel, (gz, gy, depth, cp)), out_shape=...  337 us

commit v1 on v0

--- a/solution.py
+++ b/solution.py
@@ -585,9 +585,849 @@
     return solution, norms[:CYCLES, 0]
 
 
+CROWS = 32
+PAD = 8
+
+
+def dot_parts(x, m, parts=2):
+    total = None
+    rest = x
+    for k in range(parts):
+        piece = rest.astype(jnp.bfloat16)
+        if k + 1 < parts:
+            rest = rest - piece.astype(jnp.float32)
+        term = jnp.dot(piece, m, preferred_element_type=jnp.float32)
+        total = term if total is None else total + term
+    return total
+
+
+def chain_kernel(
+    dims,
+    source, reaction, vertical, downy, upy, down2, up2, down3, down4, up3, up4,
+    out, norms,
+    v0, g0, w0, d0, v1, g1, w1, d1, raw_r, raw_s, stage, turn, lines, vsend, vrecv,
+    gx, cx, dx, win3, win4, v2, v3, v4, g3, g4, diag, fac, mask, acc, nsend, nrecv,
+    a2a_send, a2a_recv, x_send, x_recv, w3_send, w3_recv, w4_send, w4_recv,
+):
+    gz, gy, depth = dims
+    nd = gz * gy
+    zall = nd * depth
+    n0 = source.shape[1]
+    n1, n2, n3, n4 = n0 // 2, n0 // 4, n0 // 8, n0 // 16
+    r0, r1 = n0 // nd, n0 // 2 // nd
+    nt0 = n0 // 128
+    h = [COUPLING / 4.0**k for k in range(LEVELS)]
+    f32 = jnp.float32
+    a_me, b_me = lax.axis_index("gz"), lax.axis_index("gy")
+    me = a_me * gy + b_me
+    nchip = gz // 2
+
+    def bend(c):
+        return c + c // 2 - 2 * (c // 3) if nchip == 4 else c
+
+    def place(i):
+        k, core = i // 2, i % 2
+        b, q = k // nchip, k % nchip
+        q = q + (b % 2) * (nchip - 1 - 2 * q)
+        return (bend(q) * 2 + core, b)
+
+    q_me = bend(a_me // 2)
+    q_me = q_me + (b_me % 2) * (nchip - 1 - 2 * q_me)
+    p = (b_me * nchip + q_me) * 2 + a_me % 2
+    chip, par = p // 2, p % 2
+
+    def loop(lo, hi, body):
+        def step(i, c):
+            body(i)
+            return c
+        lax.fori_loop(lo, hi, step, 0)
+
+    def remote(src, dst, ss, rs, to):
+        return pltpu.make_async_remote_copy(
+            src_ref=src, dst_ref=dst, send_sem=ss, recv_sem=rs, device_id=to, device_id_type=MESH
+        )
+
+    def target(k):
+        return (p + nd + (k // 2 + k % 2) * (1 - 2 * (k % 2))) % nd
+
+    def flat(i):
+        a, b = place(i)
+        return a * gy + b
+
+    def spread(kind, src_of, dst_mine, dst_from):
+        def start(k):
+            t = target(k)
+            remote(src_of(t), dst_mine, a2a_send.at[kind, k], a2a_recv.at[kind, me], place(t)).start()
+
+        def end_send(k):
+            t = target(k)
+            remote(src_of(t), dst_mine, a2a_send.at[kind, k], a2a_recv.at[kind, me], place(t)).wait_send()
+
+        def landed(s):
+            r = dst_from(s)
+            remote(r, r, a2a_send.at[kind, 0], a2a_recv.at[kind, s], place(p)).wait_recv()
+
+        return (
+            lambda: loop(1, nd, start),
+            lambda: loop(1, nd, end_send),
+            landed,
+        )
+
+    def piece(ref, t):
+        return ref.at[:, pl.ds(r0 * t, r0), :]
+
+    def zrows(ref, s):
+        return ref.at[pl.ds(depth * s, depth)]
+
+    start_v, done_v, landed_v = spread(0, lambda t: vsend, vrecv.at[me], lambda s: vrecv.at[s])
+    start_r, done_r, landed_r = spread(
+        1, lambda t: piece(reaction, t), zrows(raw_r, me), lambda s: zrows(raw_r, s))
+    start_s, done_s, landed_s = spread(
+        2, lambda t: piece(source, t), zrows(raw_s, me), lambda s: zrows(raw_s, s))
+    start_o, done_o, landed_o = spread(
+        3, lambda t: zrows(stage, flat(t)), piece(out, p), lambda s: zrows(stage, s))
+    start_n, done_n, landed_n = spread(4, lambda t: nsend, nrecv.at[me], lambda s: nrecv.at[s])
+
+    for i in range(depth):
+        vsend[i : i + 1, :] = jnp.full((1, 128), vertical[i], f32)
+    start_v()
+    start_r()
+    start_s()
+
+    first, last = p == 0, p == nd - 1
+
+    def xchg(kind, lo_src, lo_dst, hi_src, hi_dst):
+        def down():
+            return remote(lo_src, hi_dst, x_send.at[kind, 0], x_recv.at[kind, 0], place((p + nd - 1) % nd))
+
+        def up():
+            return remote(hi_src, lo_dst, x_send.at[kind, 1], x_recv.at[kind, 1], place((p + 1) % nd))
+
+        def begin():
+            @pl.when(jnp.logical_not(first))
+            def _():
+                down().start()
+
+            @pl.when(jnp.logical_not(last))
+            def _():
+                up().start()
+
+        def end():
+            @pl.when(jnp.logical_not(first))
+            def _():
+                down().wait_send()
+                up().wait_recv()
+
+            @pl.when(jnp.logical_not(last))
+            def _():
+                up().wait_send()
+                down().wait_recv()
+
+        return begin, end
+
+    def planes0(m, dep):
+        def at(lo):
+            return v0.at[m, pl.ds(lo, dep), pl.ds(PAD, zall), :]
+        return xchg(m, at(2), at(2 - dep), at(2 + r0 - dep), at(2 + r0))
+
+    def planes1(ref, kind):
+        return xchg(kind, ref.at[pl.ds(2, 2)], ref.at[pl.ds(0, 2)],
+                    ref.at[pl.ds(r1, 2)], ref.at[pl.ds(r1 + 2, 2)])
+
+    def planes1v(m):
+        def at(lo):
+            return v1.at[m, pl.ds(lo, 2), pl.ds(PAD, zall), :]
+        return xchg(4, at(2), at(0), at(r1), at(r1 + 2))
+
+    def blocks(ref, kind):
+        return xchg(kind, ref.at[1], ref.at[0], ref.at[1], ref.at[2])
+
+    def halo_d0():
+        return xchg(5, d0.at[1], d0.at[0], d0.at[r0], d0.at[r0 + 1])
+
+    offs3 = [-1, 1, -2, 2, -3, 3]
+
+    def window3(kind):
+        buf = win3.at[kind]
+
+        def each(fn):
+            for o in offs3:
+                @pl.when(jnp.logical_and(p + o >= 0, p + o < nd))
+                def _(o=o):
+                    fn(o)
+
+        def out_of(o):
+            return remote(buf.at[3], buf.at[3 - o], w3_send.at[kind, 3 + o], w3_recv.at[kind, 3 - o],
+                          place((p + o + nd) % nd))
+
+        def begin():
+            each(lambda o: out_of(o).start())
+
+        def end():
+            def fn(o):
+                out_of(o).wait_send()
+                remote(buf.at[3 + o], buf.at[3 + o], w3_send.at[kind, 3 + o], w3_recv.at[kind, 3 + o],
+                       place(p)).wait_recv()
+            each(fn)
+
+        return begin, end
+
+    offs4 = [(o, c) for o in (0, -1, 1, -2, 2, -3, 3, -4, 4) for c in range(2)]
+
+    def window4(kind):
+        buf = win4.at[kind]
+
+        def each(fn):
+            for o, c in offs4:
+                good = par != c if o == 0 else jnp.logical_and(chip + o >= 0, chip + o < nd // 2)
+
+                @pl.when(good)
+                def _(o=o, c=c):
+                    fn(o, c)
+
+        def out_of(o, c):
+            slot = 8 + par - 2 * o
+            return remote(buf.at[8 + par], buf.at[slot], w4_send.at[kind, 8 + 2 * o + c],
+                          w4_recv.at[kind, slot], place((2 * (chip + o) + c + nd) % nd))
+
+        def begin():
+            each(lambda o, c: out_of(o, c).start())
+
+        def end():
+            def fn(o, c):
+                s = 8 + 2 * o + c
+                out_of(o, c).wait_send()
+                remote(buf.at[s], buf.at[s], w4_send.at[kind, s], w4_recv.at[kind, s], place(p)).wait_recv()
+            each(fn)
+
+        return begin, end
+
+    zpad = jnp.zeros((PAD, n0), f32)
+    for m in range(3):
+        def zero0(x, m=m):
+            v0[m, x, 0:PAD, :] = zpad
+            v0[m, x, PAD + zall : 2 * PAD + zall, :] = zpad
+        loop(0, r0 + 4, zero0)
+
+        def zero1(x, m=m):
+            v1[m, x, 0:PAD, :] = zpad[:, :n1]
+            v1[m, x, PAD + zall : 2 * PAD + zall, :] = zpad[:, :n1]
+        loop(0, r1 + 4, zero1)
+
+    tile0 = jnp.zeros((zall, 128), f32)
+    plane0 = jnp.zeros((zall, n0), f32)
+
+    def blank(lo0, x0, lo1, b):
+        for q in range(2):
+            for m in (0, 2):
+                v0[m, lo0 + q, PAD : PAD + zall, :] = plane0
+            v1[2, lo1 + q, PAD : PAD + zall, :] = tile0
+            g1[lo1 + q] = tile0
+            d1[lo1 + q] = tile0
+            w1[lo1 + q] = tile0
+        d0[x0] = plane0
+        w0[x0] = plane0
+        for k in range(CYCLES):
+            gx[k, b] = tile0
+            cx[k, b] = tile0
+        dx[b] = tile0
+
+    @pl.when(first)
+    def _():
+        blank(0, 0, 0, 0)
+
+    @pl.when(last)
+    def _():
+        blank(r0 + 2, r0 + 1, r1 + 2, 2)
+
+    for k in range(CYCLES + 1):
+        for o in offs3:
+            @pl.when(jnp.logical_or(p + o < 0, p + o >= nd))
+            def _(o=o, k=k):
+                win3[k, 3 + o] = jnp.zeros((n3 * zall // 128, 128), f32)
+        for o, c in offs4:
+            if o:
+                @pl.when(jnp.logical_or(chip + o < 0, chip + o >= nd // 2))
+                def _(o=o, c=c, k=k):
+                    win4[k, 8 + 2 * o + c] = jnp.zeros((n4 * zall // 128, 128), f32)
+    for q in range(2):
+        v2[q, 0] = tile0
+        v2[q, 4] = tile0
+        v3[q, 0] = tile0
+        v3[q, 3] = tile0
+        v4[q, 0] = tile0
+        v4[q, 3] = tile0
+    v4[1, 2] = tile0
+    acc[...] = jnp.zeros_like(acc)
+
+    lane = lax.broadcasted_iota(jnp.int32, (zall, 128), 1)
+    rows = lax.broadcasted_iota(jnp.int32, (zall, 128), 0)
+
+    for t in range(3):
+        good = [p > 0, None, p < nd - 1][t]
+        one = jnp.ones((zall, 128), f32)
+        mask[t] = one if good is None else one * good.astype(f32)
+    for t in range(2):
+        row = p - 3 + 4 * t + lane // n3
+        mask[3 + t] = jnp.where((row >= 0) & (row < nd) & (row < p + 4), 1.0, 0.0)
+        row = chip - 4 + 8 * t + lane // n4
+        mask[5 + t] = jnp.where((row >= 0) & (row < nd // 2) & (row < chip + 5), 1.0, 0.0)
+
+    def pack(rep, width):
+        k = 128 // width
+        zb = zall // k
+        part = lane[:zb]
+        got = rep[0:zb]
+        for j in range(1, k):
+            got = jnp.where(part // width == j, rep[zb * j : zb * (j + 1)], got)
+        return got
+
+    def unpack(slots, width):
+        k = 128 // width
+        zb = zall // k
+        part = lane[:zb] // width
+        parts = []
+        for j in range(k):
+            got = jnp.zeros((zb, 128), f32)
+            for s, x in enumerate(slots):
+                turn = (width * (s - j)) % 128
+                x = x if turn == 0 else pltpu.roll(x, turn, 1)
+                got = jnp.where(part == s, x, got)
+            parts.append(got)
+        return parts
+
+    def unpack3(kind, dest, add=None):
+        for t in range(2):
+            slots = [win3[kind, 4 * t + k] for k in range(4) if 4 * t + k < 7]
+            zb = zall // 4
+            for j, x in enumerate(unpack(slots, n3)):
+                if add is not None:
+                    x = x + add(j * zb, zb)
+                dest[t, j * zb : (j + 1) * zb] = x
+
+    def unpack4(kind, dest, add=None):
+        for t in range(2):
+            slots = [win4[kind, 2 * r] + win4[kind, 2 * r + 1] for r in range(8 * t, min(8 * t + 8, 9))]
+            zb = zall // 8
+            for j, x in enumerate(unpack(slots, n4)):
+                if add is not None:
+                    x = x + add(j * zb, zb)
+                dest[t, j * zb : (j + 1) * zb] = x
+
+    rawr = raw_r.reshape(zall * r0, n0)
+    raws = raw_s.reshape(zall * r0, n0)
+    staged = stage.reshape(zall * r0, n0)
+
+    def unfold(raw, j):
+        at = pl.ds(pl.multiple_of(PAD * r0 * j, PAD * r0), PAD * r0)
+        for t in range(nt0):
+            turn[t, at, :] = raw[at, 128 * t : 128 * (t + 1)]
+    raw_r[pl.ds(depth * me, depth)] = reaction[:, pl.ds(r0 * p, r0), :]
+    raw_s[pl.ds(depth * me, depth)] = source[:, pl.ds(r0 * p, r0), :]
+    vrecv[me] = vsend[...]
+    group = PAD // depth
+
+    def each_rows(landed, body):
+        def step(i):
+            j = (me // group + i) % (zall // PAD)
+            for k in range(group):
+                s = group * j + k
+
+                @pl.when(s != me)
+                def _():
+                    landed(s)
+            body(j)
+        loop(0, zall // PAD, step)
+
+    loop(0, nd, lambda s: pl.when(s != me)(lambda: landed_v(s)))
+    for s in range(nd):
+        lines[depth * s : depth * (s + 1), :] = vrecv[s]
+
+    def take_r(j):
+        z = pl.multiple_of(PAD * j, PAD)
+        unfold(rawr, j)
+        for x in range(r0):
+            for t in range(nt0):
+                d0[x + 1, pl.ds(z, PAD), 128 * t : 128 * (t + 1)] = turn[
+                    t, pl.ds(PAD * r0 * j + x, PAD, stride=r0), :]
+
+    each_rows(landed_r, take_r)
+
+    def shrink_r(i):
+        for r in range(0, zall, CROWS):
+            at = pl.ds(r, CROWS)
+            a, b = d0[2 * i + 1, at, :], d0[2 * i + 2, at, :]
+            got = dot_parts(a + b, downy[...], 3)
+            vert = lines[at, :]
+            base = 2.0 * vert + 4.0 * h[1]
+            w1[i + 2, at, :] = got
+            d = base + got
+            d1[i + 2, at, :] = d
+            base = jnp.concatenate([2.0 * vert + 4.0 * h[0]] * nt0, axis=1)
+            for k, x in ((1, a), (2, b)):
+                x = base + x
+                d0[2 * i + k, at, :] = x
+                w0[2 * i + k, at, :] = DAMPING / x
+
+    loop(0, r1, shrink_r)
+    begin_d0, end_d0 = halo_d0()
+    begin_d0()
+    begin_d1, end_d1 = planes1(d1, 6)
+    begin_d1()
+    rx2 = dot_parts(jnp.concatenate([w1[2] + w1[3], w1[4] + w1[5]], axis=1), down2[...], 3)
+    dx[1] = rx2
+    begin_dx, end_dx = blocks(dx, 7)
+    begin_dx()
+    rx3 = dot_parts(rx2, down3[...], 3)
+    win3[CYCLES, 3] = pack(rx3, n3)
+    begin_w3, end_w3 = window3(CYCLES)
+    begin_w3()
+    win4[CYCLES, 8 + par] = pack(dot_parts(rx3, down4[...], 3), n4)
+    begin_w4, end_w4 = window4(CYCLES)
+    begin_w4()
+    loop(2, r1 + 2, lambda x: w1.__setitem__(x, DAMPING / d1[x]))
+
+    def take_s(j):
+        z = pl.multiple_of(PAD * j, PAD)
+        unfold(raws, j)
+        for x in range(r0):
+            for t in range(nt0):
+                cut = slice(128 * t, 128 * (t + 1))
+                got = turn[t, pl.ds(PAD * r0 * j + x, PAD, stride=r0), :]
+                g0[x + 1, pl.ds(z, PAD), cut] = got
+                v0[0, x + 2, pl.ds(z + PAD, PAD), cut] = w0[x + 1, pl.ds(z, PAD), cut] * got
+
+    each_rows(landed_s, take_s)
+
+    ns = (zall - 1).bit_length()
+
+    def factors(f):
+        vert = lines[...]
+        a = jnp.where(rows == 0, 0.0, -vert)
+        c = jnp.where(rows == zall - 1, 0.0, -vert)
+        b = diag[f]
+        for k in range(ns):
+            s = 1 << k
+            inv = 1.0 / b
+            alpha = -a * pltpu.roll(inv, s, 0)
+            gamma = -c * pltpu.roll(inv, zall - s, 0)
+            b = b + alpha * pltpu.roll(c, s, 0) + gamma * pltpu.roll(a, zall - s, 0)
+            a = alpha * pltpu.roll(a, s, 0)
+            c = gamma * pltpu.roll(c, zall - s, 0)
+            fac[f, 2 * k] = alpha
+            fac[f, 2 * k + 1] = gamma
+        fac[f, 2 * ns] = mask[f] / b
+
+    def solve(f, right):
+        for k in range(ns):
+            s = 1 << k
+            right = (
+                right
+                + fac[f, 2 * k] * pltpu.roll(right, s, 0)
+                + fac[f, 2 * k + 1] * pltpu.roll(right, zall - s, 0)
+            )
+        return right * fac[f, 2 * ns]
+
+    def near(v, q, b, width):
+        t = v[q, b]
+        below = pltpu.roll(jnp.where(lane >= 128 - width, v[q, b - 1], t), width, 1)
+        above = pltpu.roll(jnp.where(lane < width, v[q, b + 1], t), 128 - width, 1)
+        inrow = lane % width
+        left = jnp.where(inrow == 0, 0.0, pltpu.roll(t, 1, 1))
+        right = jnp.where(inrow == width - 1, 0.0, pltpu.roll(t, 127, 1))
+        return (below + above) + (left + right)
+
+    edge = lax.broadcasted_iota(jnp.int32, (CROWS, 128), 1)
+    level0 = (v0, g0, w0, d0, nt0, h[0], 1)
+    level1 = (v1, g1, w1, d1, 1, h[1], 2)
+
+    def stencil(level, m, x, r):
+        v, g, w, d, nt, weight, go = level
+        centre, turn_r, turn_l = [], [], []
+        for t in range(nt):
+            cut = slice(128 * t, 128 * (t + 1))
+            c = v[m, x + 2, PAD + r : PAD + r + CROWS, cut]
+            centre.append(c)
+            turn_r.append(pltpu.roll(c, 1, 1))
+            turn_l.append(pltpu.roll(c, 127, 1))
+        vert = lines[r : r + CROWS, :]
+        got = []
+        for t in range(nt):
+            cut = slice(128 * t, 128 * (t + 1))
+            left = jnp.where(edge == 0, turn_r[t - 1] if t else 0.0, turn_r[t])
+            right = jnp.where(edge == 127, turn_l[t + 1] if t + 1 < nt else 0.0, turn_l[t])
+            side = (v[m, x + 1, PAD + r : PAD + r + CROWS, cut] + v[m, x + 3, PAD + r : PAD + r + CROWS, cut]) + (left + right)
+            if weight != 1.0:
+                side = weight * side
+            ends = v[m, x + 2, PAD + r - 1 : PAD + r - 1 + CROWS, cut] + v[m, x + 2, PAD + r + 1 : PAD + r + 1 + CROWS, cut]
+            got.append(g[x + go, r : r + CROWS, cut] + side + vert * ends)
+        return centre, got
+
+    def sweep_plane(level, m, q, x, record=None, put=None):
+        v, g, w, d, nt, weight, go = level
+        for r in range(0, zall, CROWS):
+            centre, got = stencil(level, m, x, r)
+            for t in range(nt):
+                cut = slice(128 * t, 128 * (t + 1))
+                wt = w[x + go, r : r + CROWS, cut]
+                if record is None:
+                    new = (1.0 - DAMPING) * centre[t] + wt * got[t]
+                else:
+                    res = got[t] - d[x + go, r : r + CROWS, cut] * centre[t]
+                    new = centre[t] + wt * res
+                    acc[record] += (res * res).reshape(CROWS // 8, 8, 128).sum(axis=0)
+                v[q, x + 2, PAD + r : PAD + r + CROWS, cut] = new
+                if put is not None:
+                    for e in range(0, CROWS, 8):
+                        put(x, r + e, t, new[e : e + 8])
+
+    def residual(level, m, x, r):
+        v, g, w, d, nt, weight, go = level
+        centre, got = stencil(level, m, x, r)
+        res = [
+            got[t] - d[x + go, r : r + CROWS, 128 * t : 128 * (t + 1)] * centre[t] for t in range(nt)]
+        return res
+
+    def sweeps(level, m, q, xs, record=None, put=None):
+        lo, hi, fn = xs
+        loop(lo, hi, lambda i: sweep_plane(level, m, q, fn(i), record, put))
+
+    def restrict0(m, lo, hi, fn):
+        def body(i):
+            i = fn(i)
+            for r in range(0, zall, CROWS):
+                a = residual(level0, m, 2 * i, r)
+                b = residual(level0, m, 2 * i + 1, r)
+                both = jnp.concatenate([s + t for s, t in zip(a, b)], axis=1)
+                g1[i + 2, r : r + CROWS, :] = dot_parts(both, downy[...])
+        loop(lo, hi, body)
+
+    def same(i):
+        return i
+
+    def rim(size, wide):
+        return lambda i: i + (i // wide) * (size - 2 * wide)
+
+    def outer(size):
+        return lambda i: -1 + i * (size + 1)
+
+    def pair0(m, q, record=None, hook=None, put=None, restrict=False):
+        begin, end = planes0(m, 2)
+        begin()
+        if hook is not None:
+            hook[0]()
+        sweeps(level0, m, 1, (1, r0 - 1, same), record)
+        if restrict:
+            restrict0(1, 1, r1 - 1, same)
+        else:
+            sweeps(level0, 1, q, (2, r0 - 2, same), None, put)
+        end()
+        if hook is not None:
+            hook[1]()
+        sweeps(level0, m, 1, (0, 2, outer(r0)))
+        sweeps(level0, m, 1, (0, 2, rim(r0, 1)), record)
+        if restrict:
+            restrict0(1, 0, 2, lambda i: i * (r1 - 1))
+        else:
+            sweeps(level0, 1, q, (0, 4, rim(r0, 2)), None, put)
+
+    def halo_factors():
+        end_dx()
+        for t in range(3):
+            diag[t] = 2.0 * lines[...] + 4.0 * h[2] + dx[t]
+        loop(0, 3, factors)
+
+    def window_factors():
+        end_w3()
+        end_w4()
+
+        def add(level):
+            return lambda r, n: 2.0 * lines[r : r + n, :] + 4.0 * h[level]
+        unpack3(CYCLES, diag.at[pl.ds(3, 2)], add(3))
+        unpack4(CYCLES, diag.at[pl.ds(5, 2)], add(4))
+        loop(3, 7, factors)
+
+    def halo_level0():
+        end_d0()
+        for x, inside in ((0, jnp.logical_not(first)), (r0 + 1, jnp.logical_not(last))):
+            @pl.when(inside)
+            def _(x=x):
+                w0[x] = DAMPING / d0[x]
+            g0[x] = v0[0, x + 1, PAD : PAD + zall, :] * d0[x] * (1.0 / DAMPING)
+
+    def halo_level1():
+        end_d1()
+        for x, inside in ((0, jnp.logical_not(first)), (r1 + 2, jnp.logical_not(last))):
+            @pl.when(inside)
+            def _(x=x):
+                for q in range(2):
+                    w1[x + q] = DAMPING / d1[x + q]
+
+    def coarse(cycle):
+        begin, end = planes1(g1, 3)
+        begin()
+        if cycle == 0:
+            window_factors()
+        loop(2, r1 + 2, lambda x: v1.__setitem__((0, x, pl.ds(PAD, zall)), w1[x] * g1[x]))
+        end()
+        if cycle == 0:
+            halo_level1()
+        for x in (0, 1, r1 + 2, r1 + 3):
+            v1[0, x, PAD : PAD + zall] = w1[x] * g1[x]
+        sweeps(level1, 0, 1, (-1, r1 + 1, same))
+
+        pairs = []
+        for i in range(r1 // 2):
+            cuts = []
+            for r in range(0, zall, CROWS):
+                a = residual(level1, 1, 2 * i, r)[0]
+                b = residual(level1, 1, 2 * i + 1, r)[0]
+                cuts.append(a + b)
+            pairs.append(jnp.concatenate(cuts, axis=0))
+        gx[cycle, 1] = dot_parts(jnp.concatenate(pairs, axis=1), down2[...])
+        e2 = lines2(cycle)
+
+        for i in range(r1 // 2):
+            e = dot_parts(e2, up2[i])
+            for x in (2 * i, 2 * i + 1):
+                v1[2, x + 2, PAD : PAD + zall] = v1[1, x + 2, PAD : PAD + zall] + e
+        begin, end = planes1v(2)
+        begin()
+        sweeps(level1, 2, 1, (1, r1 - 1, same))
+        end()
+        sweeps(level1, 2, 1, (0, 2, outer(r1)))
+        sweeps(level1, 2, 1, (0, 2, rim(r1, 1)))
+        sweeps(level1, 1, 0, (0, r1, same))
+
+    def lines_sweep(v, q, s, lo, hi, right, f, weight, width):
+        loop(lo, hi, lambda b: v.__setitem__(
+            (s, b), solve(f + b - 1, right[b - 1] + weight * near(v, q, b, width))))
+
+    def line_residual(v, q, b, right, f, weight, width):
+        values = v[q, b]
+        before = jnp.where(rows == 0, 0.0, pltpu.roll(values, 1, 0))
+        after = jnp.where(rows == zall - 1, 0.0, pltpu.roll(values, zall - 1, 0))
+        return right[b - 1] + weight * near(v, q, b, width) + lines[...] * (before + after) - diag[f + b - 1] * values
+
+    def lines2(cycle):
+        right = gx.at[cycle]
+        begin, end = blocks(right, 8 + cycle)
+        begin()
+        v2[0, 2] = solve(1, right[1])
+        end()
+        loop(0, 2, lambda i: v2.__setitem__((0, 1 + 2 * i), solve(2 * i, right[2 * i])))
+        lines_sweep(v2, 0, 1, 1, 4, right, 0, h[2], n2)
+        res = line_residual(v2, 1, 2, right, 0, h[2], n2)
+        win3[cycle, 3] = pack(dot_parts(res, down3[...]), n3)
+        e3 = lines3(cycle)
+        cx[cycle, 1] = v2[1, 2] + dot_parts(e3, up3[...])
+        begin, end = blocks(cx.at[cycle], 8 + CYCLES + cycle)
+        begin()
+        end()
+        for b in range(3):
+            v2[0, b + 1] = cx[cycle, b]
+        lines_sweep(v2, 0, 1, 1, 4, right, 0, h[2], n2)
+        return solve(1, right[1] + h[2] * near(v2, 1, 2, n2))
+
+    def lines3(cycle):
+        begin, end = window3(cycle)
+        begin()
+        end()
+        unpack3(cycle, g3)
+        loop(1, 3, lambda b: v3.__setitem__((0, b), solve(3 + b - 1, g3[b - 1])))
+        lines_sweep(v3, 0, 1, 1, 3, g3, 3, h[3], n3)
+        res = line_residual(v3, 1, 1, g3, 3, h[3], n3)
+        win4[cycle, 8 + par] = pack(dot_parts(res, down4[...]), n4)
+        e4 = lines4(cycle)
+        for t in range(2):
+            v3[0, t + 1] = v3[1, t + 1] + dot_parts(e4, up4[par, t])
+        lines_sweep(v3, 0, 1, 1, 3, g3, 3, h[3], n3)
+        return solve(3, g3[0] + h[3] * near(v3, 1, 1, n3))
+
+    def lines4(cycle):
+        begin, end = window4(cycle)
+        begin()
+        end()
+        unpack4(cycle, g4)
+        loop(1, 3, lambda b: v4.__setitem__((0, b), solve(5 + b - 1, g4[b - 1])))
+        q = 0
+        for k in range(1, COARSE - 1):
+            v4[1 - q, 1] = solve(5, g4[0] + h[4] * near(v4, q, 1, n4))
+            q = 1 - q
+        return solve(5, g4[0] + h[4] * near(v4, q, 1, n4))
+
+    def correct0(m, q, lo, hi, fn):
+        def body(i):
+            i = fn(i)
+            for r in range(0, zall, CROWS):
+                e = dot_parts(v1[0, i + 2, PAD + r : PAD + r + CROWS, :], upy[...])
+                for x in (2 * i + 2, 2 * i + 3):
+                    v0[q, x, PAD + r : PAD + r + CROWS, :] = v0[m, x, PAD + r : PAD + r + CROWS, :] + e
+        loop(lo, hi, body)
+
+    def put(x, z, t, value):
+        turn[t, pl.ds(z * r0 + x, 8, stride=r0), :] = value
+
+    def fold(j):
+        at = pl.ds(pl.multiple_of(PAD * r0 * j, PAD * r0), PAD * r0)
+        for t in range(nt0):
+            staged[at, 128 * t : 128 * (t + 1)] = turn[t, at, :]
+
+    pair0(0, 1, hook=(halo_factors, halo_level0), restrict=True)
+    coarse(0)
+    correct0(1, 2, 0, r1, same)
+    pair0(2, 0)
+    pair0(0, 2, record=0)
+    begin, end = planes0(2, 1)
+    begin()
+    restrict0(2, 1, r1 - 1, same)
+    end()
+    restrict0(2, 0, 2, lambda i: i * (r1 - 1))
+    coarse(1)
+    correct0(2, 0, 0, r1, same)
+    pair0(0, 2, put=put)
+    loop(0, zall // PAD, fold)
+    begin, end = planes0(2, 1)
+    begin()
+    start_o()
+    out[:, pl.ds(r0 * p, r0), :] = stage[pl.ds(depth * me, depth)]
+
+    def last_norm(x):
+        for r in range(0, zall, CROWS):
+            for res in residual(level0, 2, x, r):
+                acc[CYCLES - 1] += (res * res).reshape(CROWS // 8, 8, 128).sum(axis=0)
+
+    loop(1, r0 - 1, last_norm)
+    end()
+    loop(0, 2, lambda i: last_norm(i * (r0 - 1)))
+    ridx = lax.broadcasted_iota(jnp.int32, (8, 128), 0)
+    part = jnp.zeros((8, 128), f32)
+    for k in range(CYCLES):
+        part = jnp.where(ridx == k, jnp.sum(acc[k]), part)
+    nsend[...] = part
+    start_n()
+    total = part
+    done_v()
+    done_r()
+    done_s()
+
+    def finish(s):
+        @pl.when(s != me)
+        def _():
+            landed_n(s)
+            remote(zrows(stage, 0), zrows(stage, 0), a2a_send.at[3, 0], a2a_recv.at[3, s], place(p)).wait_recv()
+    loop(0, nd, finish)
+    nrecv[me] = part
+    total = jnp.sum(nrecv[...], axis=0)
+    norms[...] = total * (1.0 / (zall * n0 * n0))
+    done_o()
+    done_n()
+
+
+def chain_shards(gz, gy, source, vertical, reaction):
+    depth, n0 = source.shape[0], source.shape[1]
+    nd = gz * gy
+    zall = nd * depth
+    n1, n2, n3, n4 = n0 // 2, n0 // 4, n0 // 8, n0 // 16
+    r0, r1 = n0 // nd, n1 // nd
+    f32 = jnp.float32
+    bf16 = jnp.bfloat16
+
+    def halve(n, k):
+        return np.tile((np.arange(n)[:, None] // 2 == np.arange(n // 2)[None, :]).astype(np.float32) * 0.25, (1, k))
+
+    downy = halve(n0, 1)
+    upy = halve(n0, 1).T * 4.0
+    down2 = np.zeros((r1 // 2 * n1, 128), np.float32)
+    up2 = np.zeros((r1 // 2, 128, n1), np.float32)
+    down3 = np.zeros((128, 128), np.float32)
+    up3 = np.zeros((128, 128), np.float32)
+    for i in range(r1 // 2):
+        down2[i * n1 : (i + 1) * n1, i * n2 : (i + 1) * n2] = halve(n1, 1)
+        up2[i, i * n2 : (i + 1) * n2, :] = halve(n1, 1).T * 4.0
+        down3[i * n2 : (i + 1) * n2] = halve(n2, 128 // n3)
+        up3[3 * n3 : 4 * n3, i * n2 : (i + 1) * n2] = halve(n2, 1).T * 4.0
+    down4 = np.zeros((128, 128), np.float32)
+    down4[3 * n3 : 4 * n3] = halve(n3, 128 // n4)
+    up4 = np.zeros((2, 2, 128, 128), np.float32)
+    for par in range(2):
+        for s in range(1, 6):
+            r = 4 + (par - 3 + s) // 2
+            up4[par, s // 4, r * n4 : (r + 1) * n4, s % 4 * n3 : (s % 4 + 1) * n3] = halve(n3, 1).T * 4.0
+    consts = [jnp.asarray(c, bf16) for c in (downy, upy, down2, up2, down3, down4, up3, up4)]
+    vm = pl.BlockSpec(memory_space=pltpu.VMEM)
+    sm = pl.BlockSpec(memory_space=pltpu.SMEM)
+    ns = (zall - 1).bit_length()
+    dma = pltpu.SemaphoreType.DMA
+    solution, norms = pl.pallas_call(
+        functools.partial(chain_kernel, (gz, gy, depth)),
+        out_shape=(
+            jax.ShapeDtypeStruct(source.shape, f32),
+            jax.ShapeDtypeStruct((8, 128), f32),
+        ),
+        in_specs=[vm, vm, sm] + [vm] * len(consts),
+        out_specs=(vm, vm),
+        scratch_shapes=[
+            pltpu.VMEM((3, r0 + 4, zall + 2 * PAD, n0), f32),
+            pltpu.VMEM((r0 + 2, zall, n0), f32),
+            pltpu.VMEM((r0 + 2, zall, n0), f32),
+            pltpu.VMEM((r0 + 2, zall, n0), f32),
+            pltpu.VMEM((3, r1 + 4, zall + 2 * PAD, n1), f32),
+            pltpu.VMEM((r1 + 4, zall, n1), f32),
+            pltpu.VMEM((r1 + 4, zall, n1), f32),
+            pltpu.VMEM((r1 + 4, zall, n1), f32),
+            pltpu.VMEM((zall, r0, n0), f32),
+            pltpu.VMEM((zall, r0, n0), f32),
+            pltpu.VMEM((zall, r0, n0), f32),
+            pltpu.VMEM((n0 // 128, zall * r0, 128), f32),
+            pltpu.VMEM((zall, 128), f32),
+            pltpu.VMEM((depth, 128), f32),
+            pltpu.VMEM((nd, depth, 128), f32),
+            pltpu.VMEM((CYCLES, 3, zall, 128), f32),
+            pltpu.VMEM((CYCLES, 3, zall, 128), f32),
+            pltpu.VMEM((3, zall, 128), f32),
+            pltpu.VMEM((CYCLES + 1, 7, n3 * zall // 128, 128), f32),
+            pltpu.VMEM((CYCLES + 1, 18, n4 * zall // 128, 128), f32),
+            pltpu.VMEM((2, 5, zall, 128), f32),
+            pltpu.VMEM((2, 4, zall, 128), f32),
+            pltpu.VMEM((2, 4, zall, 128), f32),
+            pltpu.VMEM((2, zall, 128), f32),
+            pltpu.VMEM((2, zall, 128), f32),
+            pltpu.VMEM((7, zall, 128), f32),
+            pltpu.VMEM((7, 2 * ns + 1, zall, 128), f32),
+            pltpu.VMEM((7, zall, 128), f32),
+            pltpu.VMEM((CYCLES, 8, 128), f32),
+            pltpu.VMEM((8, 128), f32),
+            pltpu.VMEM((nd, 8, 128), f32),
+            dma((5, nd)),
+            dma((5, nd)),
+            dma((8 + 2 * CYCLES, 2)),
+            dma((8 + 2 * CYCLES, 2)),
+            dma((CYCLES + 1, 7)),
+            dma((CYCLES + 1, 7)),
+            dma((CYCLES + 1, 18)),
+            dma((CYCLES + 1, 18)),
+        ],
+        compiler_params=pltpu.CompilerParams(
+            has_side_effects=True, vmem_limit_bytes=64000 * 1024
+        ),
+    )(source, reaction, vertical, *consts)
+    return solution, norms[:CYCLES, 0]
+
+
+def shards_of(gz, gy, source, vertical, reaction):
+    depth, n0 = source.shape[0], source.shape[1]
+    nd = gz * gy
+    fits = (
+        gz % 2 == 0 and n0 % (8 * nd) == 0 and n0 // nd == 8 and n0 % 256 == 0 and n0 // 4 * 2 == 128
+        and PAD % depth == 0 and nd * depth % 128 == 0 and (LEVELS, SWITCH, SWEEPS, COARSE, CYCLES) == (5, 2, 2, 4, 2)
+    )
+    return (chain_shards if fits else shards)(gz, gy, source, vertical, reaction)
+
+
 def solution(mesh):
     return jax.shard_map(
-        functools.partial(shards, mesh.shape["gz"], mesh.shape["gy"]),
+        functools.partial(shards_of, mesh.shape["gz"], mesh.shape["gy"]),
         mesh=mesh,
         in_specs=(P(("gz", "gy"), None, None), P(("gz", "gy")), P(("gz", "gy"), None, None)),
         out_specs=(P(("gz", "gy"), None, None), P()),

time: 342 us -> 190 us (0.56)
  Pallas kernels: 337 us -> 185 us
    pallas_call x1, Pallas kernels: 337 us -> 185 us  [chain_shards(): pl.pallas_call(functools.partial(chain_kernel, (gz, gy, depth)), out_shap...]
where the time goes in v1:
time: 190 us; the launch traced here: 189 us
  Pallas kernels  185 us (97%)
  local copies, waits for them, and re-layouts  3.59 us (2%)
    pallas_call x1, Pallas kernels, chain_shards(): pl.pallas_call(functools.partial(chain_kernel, (gz, gy, depth)), out_shap...  185 us

profile of v1, /device:TPU:0, one launch (start us, length us, event | category | flops | bytes accessed | tf_op | source)
XLA Modules:
  0.0 189.3 jit_solution(15962585786593853914)
XLA Ops:
  0.6 185.1 %shard_map.122 = (f32[4,256,256]{2,1,0:T(8,128)}, f32[8,128]{1,0:T(8,128)}) custom-call(f32[4,256,256]{2,1,0:T(8,128)} %source.1, f32[4,256,256]{2,1,0:T(8,128)} %reaction.1, f32[4]{0:T(128)} %vertical.1, bf16[256,128]{1,0:T(8,128)(2,1)} %constant.14.clone.downy.down2, bf16[128,256]{1,0:T(8,128)(2,1)} %constant.15.clone.upy, ...), custom_call_target="tpu_custom_call" | custom-call | tf_op jit(solution)/shard_map/pallas_call | solution.py:1362
  185.7 1.3 slice_reduce_fusion
  187.0 2.3 %copy.14 = f32[4,256,256]{2,1,0:T(8,128)} copy(f32[4,256,256]{2,1,0:T(8,128)} %get-tuple-element.8) | data formatting | bytes 2097152

commit v2 on v1

--- a/solution.py
+++ b/solution.py
@@ -586,6 +586,7 @@
 
 
 CROWS = 32
+VMEM_LIMIT = 64000 * 1024
 PAD = 8
 
 
@@ -603,11 +604,12 @@
 
 def chain_kernel(
     dims,
-    source, reaction, vertical, downy, upy, down2, up2, down3, down4, up3, up4,
+    source_in, reaction_in, vertical,
     out, norms,
+    source, reaction, downy, upy, up2, down3, down4, up3, up4, load,
     v0, g0, w0, d0, v1, g1, w1, d1, raw_r, raw_s, stage, turn, lines, vsend, vrecv,
     gx, cx, dx, win3, win4, v2, v3, v4, g3, g4, diag, fac, mask, acc, nsend, nrecv,
-    a2a_send, a2a_recv, x_send, x_recv, w3_send, w3_recv, w4_send, w4_recv,
+    a2a_send, a2a_recv, from_sem, x_send, x_recv, w3_send, w3_recv, w4_send, w4_recv,
 ):
     gz, gy, depth = dims
     nd = gz * gy
@@ -654,24 +656,24 @@
         a, b = place(i)
         return a * gy + b
 
-    def spread(kind, src_of, dst_mine, dst_from):
+    def spread(kind, src_of, dst_mine, whole, each=None):
         def start(k):
             t = target(k)
-            remote(src_of(t), dst_mine, a2a_send.at[kind, k], a2a_recv.at[kind, me], place(t)).start()
-
-        def end_send(k):
-            t = target(k)
-            remote(src_of(t), dst_mine, a2a_send.at[kind, k], a2a_recv.at[kind, me], place(t)).wait_send()
+            sem = a2a_recv.at[kind] if each is None else from_sem.at[me]
+            remote(src_of(t), dst_mine, a2a_send.at[kind], sem, place(t)).start()
+
+        def wait_all(recv):
+            copy = remote(whole, whole, a2a_send.at[kind], a2a_recv.at[kind], place(p))
+            copy.wait_recv() if recv else copy.wait_send()
 
         def landed(s):
-            r = dst_from(s)
-            remote(r, r, a2a_send.at[kind, 0], a2a_recv.at[kind, s], place(p)).wait_recv()
-
-        return (
-            lambda: loop(1, nd, start),
-            lambda: loop(1, nd, end_send),
-            landed,
-        )
+            if each is None:
+                wait_all(True)
+            else:
+                r = each(s)
+                remote(r, r, a2a_send.at[kind], from_sem.at[s], place(p)).wait_recv()
+
+        return lambda: loop(1, nd, start), lambda: wait_all(False), landed
 
     def piece(ref, t):
         return ref.at[:, pl.ds(r0 * t, r0), :]
@@ -679,20 +681,46 @@
     def zrows(ref, s):
         return ref.at[pl.ds(depth * s, depth)]
 
-    start_v, done_v, landed_v = spread(0, lambda t: vsend, vrecv.at[me], lambda s: vrecv.at[s])
-    start_r, done_r, landed_r = spread(
-        1, lambda t: piece(reaction, t), zrows(raw_r, me), lambda s: zrows(raw_r, s))
+    zrest = pl.ds(0, depth * (nd - 1))
+    rest = pl.ds(0, nd - 1)
+    start_v, done_v, landed_v = spread(0, lambda t: vsend, vrecv.at[me], vrecv.at[rest])
+    start_r, done_r, landed_r = spread(1, lambda t: piece(reaction, t), zrows(raw_r, me), raw_r.at[zrest])
     start_s, done_s, landed_s = spread(
-        2, lambda t: piece(source, t), zrows(raw_s, me), lambda s: zrows(raw_s, s))
+        2, lambda t: piece(source, t), zrows(raw_s, me), raw_s.at[zrest], lambda s: zrows(raw_s, s))
     start_o, done_o, landed_o = spread(
-        3, lambda t: zrows(stage, flat(t)), piece(out, p), lambda s: zrows(stage, s))
-    start_n, done_n, landed_n = spread(4, lambda t: nsend, nrecv.at[me], lambda s: nrecv.at[s])
-
+        3, lambda t: zrows(stage, flat(t)), piece(out, p), stage.at[zrest], lambda s: zrows(stage, s))
+    start_n, done_n, landed_n = spread(4, lambda t: nsend, nrecv.at[me], nrecv.at[rest])
+
+    load_r = pltpu.make_async_copy(reaction_in, reaction, load.at[0])
+    load_s = pltpu.make_async_copy(source_in, source, load.at[1])
+    load_r.start()
+    load_s.start()
     for i in range(depth):
         vsend[i : i + 1, :] = jnp.full((1, 128), vertical[i], f32)
+    load_r.wait()
+    start_r()
     start_v()
-    start_r()
+    load_s.wait()
     start_s()
+
+    def fill(ref, at, value):
+        shape = ref.shape[-2:]
+        row = lax.broadcasted_iota(jnp.int32, shape, 0)
+        col = lax.broadcasted_iota(jnp.int32, shape, 1)
+        hit, scale = value(row, col)
+        ref[at] = jnp.where(hit, scale, 0.0).astype(jnp.bfloat16)
+
+    fill(downy, ..., lambda r, c: (r // 2 == c, 0.25))
+    fill(upy, ..., lambda r, c: (r == c // 2, 1.0))
+    for i in range(r1 // 2):
+        fill(up2, i, lambda r, c: (r == n2 * i + c // 2, 1.0))
+    fill(down3, ..., lambda r, c: (r % n2 // 2 == c % n3, 0.25))
+    fill(down4, 0, lambda r, c: ((r >= 3 * n3) & ((r - 3 * n3) // 2 == c % n4), 0.25))
+    fill(down4, 1, lambda r, c: ((r < n3) & (r // 2 == c % n4), 0.25))
+    fill(up3, 0, lambda r, c: (r == 3 * n3 + c % n2 // 2, 1.0))
+    fill(up3, 1, lambda r, c: (r == c % n2 // 2, 1.0))
+    for t in range(2):
+        fill(up4, t, lambda r, c: (r == n4 * (4 + (4 * t + c // n3 + 5) // 2 - 4) + c % n3 // 2, 1.0))
 
     first, last = p == 0, p == nd - 1
 
@@ -745,20 +773,63 @@
     def halo_d0():
         return xchg(5, d0.at[1], d0.at[0], d0.at[r0], d0.at[r0 + 1])
 
-    offs3 = [-1, 1, -2, 2, -3, 3]
+    offs3 = [(o, c) for o in (0, -1, 1, -2, 2) for c in range(2)]
 
     def window3(kind):
         buf = win3.at[kind]
 
+        def out_of(o, c):
+            slot = par + 3 - 2 * o
+            return remote(buf.at[3 + par], buf.at[slot], w3_send.at[4 + 2 * o + c], w3_recv.at[kind // CYCLES, slot],
+                          place((2 * (chip + o) + c + nd) % nd))
+
+        def goes(o, c):
+            there = jnp.logical_and(chip + o >= 0, chip + o < nd // 2)
+            if o == 0:
+                return par != c
+            if o == -2:
+                return jnp.logical_and(there, par == 0)
+            if o == 2:
+                return jnp.logical_and(there, par == 1)
+            return there
+
+        def begin():
+            for o, c in offs3:
+                @pl.when(goes(o, c))
+                def _(o=o, c=c):
+                    out_of(o, c).start()
+
+        def end():
+            for o, c in offs3:
+                @pl.when(goes(o, c))
+                def _(o=o, c=c):
+                    out_of(o, c).wait_send()
+            for q in range(8):
+                row = 2 * chip - 3 + q
+                inside = jnp.logical_and(row >= 0, row < nd)
+                if q in (3, 4):
+                    inside = par != q - 3
+
+                @pl.when(inside)
+                def _(q=q):
+                    remote(buf.at[q], buf.at[q], w3_send.at[0], w3_recv.at[kind // CYCLES, q], place(p)).wait_recv()
+
+        return begin, end
+
+    offs4 = [-1, 1, -2, 2, -3, 3, -4, 4]
+
+    def window4(kind):
+        buf = win4.at[kind]
+
         def each(fn):
-            for o in offs3:
-                @pl.when(jnp.logical_and(p + o >= 0, p + o < nd))
+            for o in offs4:
+                @pl.when(jnp.logical_and(chip + o >= 0, chip + o < nd // 2))
                 def _(o=o):
                     fn(o)
 
         def out_of(o):
-            return remote(buf.at[3], buf.at[3 - o], w3_send.at[kind, 3 + o], w3_recv.at[kind, 3 - o],
-                          place((p + o + nd) % nd))
+            return remote(buf.at[4], buf.at[4 - o], w4_send.at[4 + o], w4_recv.at[kind // CYCLES, 4 - o],
+                          place((p + 2 * o + nd) % nd))
 
         def begin():
             each(lambda o: out_of(o).start())
@@ -766,38 +837,8 @@
         def end():
             def fn(o):
                 out_of(o).wait_send()
-                remote(buf.at[3 + o], buf.at[3 + o], w3_send.at[kind, 3 + o], w3_recv.at[kind, 3 + o],
+                remote(buf.at[4 + o], buf.at[4 + o], w4_send.at[4 + o], w4_recv.at[kind // CYCLES, 4 + o],
                        place(p)).wait_recv()
-            each(fn)
-
-        return begin, end
-
-    offs4 = [(o, c) for o in (0, -1, 1, -2, 2, -3, 3, -4, 4) for c in range(2)]
-
-    def window4(kind):
-        buf = win4.at[kind]
-
-        def each(fn):
-            for o, c in offs4:
-                good = par != c if o == 0 else jnp.logical_and(chip + o >= 0, chip + o < nd // 2)
-
-                @pl.when(good)
-                def _(o=o, c=c):
-                    fn(o, c)
-
-        def out_of(o, c):
-            slot = 8 + par - 2 * o
-            return remote(buf.at[8 + par], buf.at[slot], w4_send.at[kind, 8 + 2 * o + c],
-                          w4_recv.at[kind, slot], place((2 * (chip + o) + c + nd) % nd))
-
-        def begin():
-            each(lambda o, c: out_of(o, c).start())
-
-        def end():
-            def fn(o, c):
-                s = 8 + 2 * o + c
-                out_of(o, c).wait_send()
-                remote(buf.at[s], buf.at[s], w4_send.at[kind, s], w4_recv.at[kind, s], place(p)).wait_recv()
             each(fn)
 
         return begin, end
@@ -841,15 +882,14 @@
         blank(r0 + 2, r0 + 1, r1 + 2, 2)
 
     for k in range(CYCLES + 1):
-        for o in offs3:
-            @pl.when(jnp.logical_or(p + o < 0, p + o >= nd))
+        for q in range(8):
+            @pl.when(jnp.logical_or(2 * chip - 3 + q < 0, 2 * chip - 3 + q >= nd))
+            def _(q=q, k=k):
+                win3[k, q] = jnp.zeros((n3 * zall // 128, 128), f32)
+        for o in offs4:
+            @pl.when(jnp.logical_or(chip + o < 0, chip + o >= nd // 2))
             def _(o=o, k=k):
-                win3[k, 3 + o] = jnp.zeros((n3 * zall // 128, 128), f32)
-        for o, c in offs4:
-            if o:
-                @pl.when(jnp.logical_or(chip + o < 0, chip + o >= nd // 2))
-                def _(o=o, c=c, k=k):
-                    win4[k, 8 + 2 * o + c] = jnp.zeros((n4 * zall // 128, 128), f32)
+                win4[k, 4 + o] = jnp.zeros((n4 * zall // 128, 128), f32)
     for q in range(2):
         v2[q, 0] = tile0
         v2[q, 4] = tile0
@@ -868,8 +908,8 @@
         one = jnp.ones((zall, 128), f32)
         mask[t] = one if good is None else one * good.astype(f32)
     for t in range(2):
-        row = p - 3 + 4 * t + lane // n3
-        mask[3 + t] = jnp.where((row >= 0) & (row < nd) & (row < p + 4), 1.0, 0.0)
+        row = 2 * chip - 3 + 4 * t + lane // n3
+        mask[3 + t] = jnp.where((row >= 0) & (row < nd), 1.0, 0.0)
         row = chip - 4 + 8 * t + lane // n4
         mask[5 + t] = jnp.where((row >= 0) & (row < nd // 2) & (row < chip + 5), 1.0, 0.0)
 
@@ -898,7 +938,7 @@
 
     def unpack3(kind, dest, add=None):
         for t in range(2):
-            slots = [win3[kind, 4 * t + k] for k in range(4) if 4 * t + k < 7]
+            slots = [win3[kind, 4 * t + k] for k in range(4)]
             zb = zall // 4
             for j, x in enumerate(unpack(slots, n3)):
                 if add is not None:
@@ -907,7 +947,7 @@
 
     def unpack4(kind, dest, add=None):
         for t in range(2):
-            slots = [win4[kind, 2 * r] + win4[kind, 2 * r + 1] for r in range(8 * t, min(8 * t + 8, 9))]
+            slots = [win4[kind, r] for r in range(8 * t, min(8 * t + 8, 9))]
             zb = zall // 8
             for j, x in enumerate(unpack(slots, n4)):
                 if add is not None:
@@ -930,7 +970,7 @@
     def each_rows(landed, body):
         def step(i):
             j = (me // group + i) % (zall // PAD)
-            for k in range(group):
+            for k in range(group if landed is not None else 0):
                 s = group * j + k
 
                 @pl.when(s != me)
@@ -939,7 +979,7 @@
             body(j)
         loop(0, zall // PAD, step)
 
-    loop(0, nd, lambda s: pl.when(s != me)(lambda: landed_v(s)))
+    landed_v(None)
     for s in range(nd):
         lines[depth * s : depth * (s + 1), :] = vrecv[s]
 
@@ -951,7 +991,8 @@
                 d0[x + 1, pl.ds(z, PAD), 128 * t : 128 * (t + 1)] = turn[
                     t, pl.ds(PAD * r0 * j + x, PAD, stride=r0), :]
 
-    each_rows(landed_r, take_r)
+    landed_r(None)
+    each_rows(None, take_r)
 
     def shrink_r(i):
         for r in range(0, zall, CROWS):
@@ -974,17 +1015,15 @@
     begin_d0()
     begin_d1, end_d1 = planes1(d1, 6)
     begin_d1()
-    rx2 = dot_parts(jnp.concatenate([w1[2] + w1[3], w1[4] + w1[5]], axis=1), down2[...], 3)
+    rx2 = dot_parts(jnp.concatenate([w1[2] + w1[3], w1[4] + w1[5]], axis=1), downy[...], 3)
     dx[1] = rx2
     begin_dx, end_dx = blocks(dx, 7)
     begin_dx()
     rx3 = dot_parts(rx2, down3[...], 3)
-    win3[CYCLES, 3] = pack(rx3, n3)
+    win3[CYCLES, 3 + par] = pack(rx3, n3)
     begin_w3, end_w3 = window3(CYCLES)
     begin_w3()
-    win4[CYCLES, 8 + par] = pack(dot_parts(rx3, down4[...], 3), n4)
     begin_w4, end_w4 = window4(CYCLES)
-    begin_w4()
     loop(2, r1 + 2, lambda x: w1.__setitem__(x, DAMPING / d1[x]))
 
     def take_s(j):
@@ -1111,9 +1150,11 @@
     def outer(size):
         return lambda i: -1 + i * (size + 1)
 
-    def pair0(m, q, record=None, hook=None, put=None, restrict=False):
+    def pair0(m, q, record=None, hook=None, put=None, restrict=False, before=None):
         begin, end = planes0(m, 2)
         begin()
+        if before is not None:
+            before()
         if hook is not None:
             hook[0]()
         sweeps(level0, m, 1, (1, r0 - 1, same), record)
@@ -1136,16 +1177,21 @@
         for t in range(3):
             diag[t] = 2.0 * lines[...] + 4.0 * h[2] + dx[t]
         loop(0, 3, factors)
+        end_w3()
+        unpack3(CYCLES, g3)
+        win4[CYCLES, 4] = pack(
+            dot_parts(g3[0], down4[0], 3) + dot_parts(g3[1], down4[1], 3), n4)
+        begin_w4()
 
     def window_factors():
-        end_w3()
-        end_w4()
-
         def add(level):
             return lambda r, n: 2.0 * lines[r : r + n, :] + 4.0 * h[level]
-        unpack3(CYCLES, diag.at[pl.ds(3, 2)], add(3))
+        for t in range(2):
+            diag[3 + t] = 2.0 * lines[...] + 4.0 * h[3] + g3[t]
+        loop(3, 5, factors)
+        end_w4()
         unpack4(CYCLES, diag.at[pl.ds(5, 2)], add(4))
-        loop(3, 7, factors)
+        loop(5, 7, factors)
 
     def halo_level0():
         end_d0()
@@ -1184,7 +1230,7 @@
                 b = residual(level1, 1, 2 * i + 1, r)[0]
                 cuts.append(a + b)
             pairs.append(jnp.concatenate(cuts, axis=0))
-        gx[cycle, 1] = dot_parts(jnp.concatenate(pairs, axis=1), down2[...])
+        gx[cycle, 1] = dot_parts(jnp.concatenate(pairs, axis=1), downy[...])
         e2 = lines2(cycle)
 
         for i in range(r1 // 2):
@@ -1211,17 +1257,17 @@
 
     def lines2(cycle):
         right = gx.at[cycle]
-        begin, end = blocks(right, 8 + cycle)
+        begin, end = blocks(right, 8)
         begin()
         v2[0, 2] = solve(1, right[1])
         end()
         loop(0, 2, lambda i: v2.__setitem__((0, 1 + 2 * i), solve(2 * i, right[2 * i])))
         lines_sweep(v2, 0, 1, 1, 4, right, 0, h[2], n2)
         res = line_residual(v2, 1, 2, right, 0, h[2], n2)
-        win3[cycle, 3] = pack(dot_parts(res, down3[...]), n3)
+        win3[cycle, 3 + par] = pack(dot_parts(res, down3[...]), n3)
         e3 = lines3(cycle)
-        cx[cycle, 1] = v2[1, 2] + dot_parts(e3, up3[...])
-        begin, end = blocks(cx.at[cycle], 8 + CYCLES + cycle)
+        cx[cycle, 1] = v2[1, 2] + dot_parts(e3, up3[par])
+        begin, end = blocks(cx.at[cycle], 9)
         begin()
         end()
         for b in range(3):
@@ -1236,13 +1282,16 @@
         unpack3(cycle, g3)
         loop(1, 3, lambda b: v3.__setitem__((0, b), solve(3 + b - 1, g3[b - 1])))
         lines_sweep(v3, 0, 1, 1, 3, g3, 3, h[3], n3)
-        res = line_residual(v3, 1, 1, g3, 3, h[3], n3)
-        win4[cycle, 8 + par] = pack(dot_parts(res, down4[...]), n4)
+        both = None
+        for t in range(2):
+            part = dot_parts(line_residual(v3, 1, t + 1, g3, 3, h[3], n3), down4[t])
+            both = part if both is None else both + part
+        win4[cycle, 4] = pack(both, n4)
         e4 = lines4(cycle)
         for t in range(2):
-            v3[0, t + 1] = v3[1, t + 1] + dot_parts(e4, up4[par, t])
+            v3[0, t + 1] = v3[1, t + 1] + dot_parts(e4, up4[t])
         lines_sweep(v3, 0, 1, 1, 3, g3, 3, h[3], n3)
-        return solve(3, g3[0] + h[3] * near(v3, 1, 1, n3))
+        return solve(3 + par, g3[par] + h[3] * near(v3, 1, 1 + par, n3))
 
     def lines4(cycle):
         begin, end = window4(cycle)
@@ -1275,8 +1324,8 @@
 
     pair0(0, 1, hook=(halo_factors, halo_level0), restrict=True)
     coarse(0)
-    correct0(1, 2, 0, r1, same)
-    pair0(2, 0)
+    correct0(1, 2, 0, 2, lambda i: i * (r1 - 1))
+    pair0(2, 0, before=lambda: correct0(1, 2, 1, r1 - 1, same))
     pair0(0, 2, record=0)
     begin, end = planes0(2, 1)
     begin()
@@ -1284,13 +1333,14 @@
     end()
     restrict0(2, 0, 2, lambda i: i * (r1 - 1))
     coarse(1)
-    correct0(2, 0, 0, r1, same)
-    pair0(0, 2, put=put)
+    correct0(2, 0, 0, 2, lambda i: i * (r1 - 1))
+    pair0(0, 2, put=put, before=lambda: correct0(2, 0, 1, r1 - 1, same))
     loop(0, zall // PAD, fold)
     begin, end = planes0(2, 1)
     begin()
     start_o()
-    out[:, pl.ds(r0 * p, r0), :] = stage[pl.ds(depth * me, depth)]
+    keep = pltpu.make_async_copy(zrows(stage, me), piece(out, p), load.at[2])
+    keep.start()
 
     def last_norm(x):
         for r in range(0, zall, CROWS):
@@ -1314,12 +1364,14 @@
     def finish(s):
         @pl.when(s != me)
         def _():
-            landed_n(s)
-            remote(zrows(stage, 0), zrows(stage, 0), a2a_send.at[3, 0], a2a_recv.at[3, s], place(p)).wait_recv()
+            landed_o(s)
     loop(0, nd, finish)
+    landed_n(None)
     nrecv[me] = part
     total = jnp.sum(nrecv[...], axis=0)
-    norms[...] = total * (1.0 / (zall * n0 * n0))
+    for k in range(CYCLES):
+        norms[k] = total[k, 0] * (1.0 / (zall * n0 * n0))
+    keep.wait()
     done_o()
     done_n()
 
@@ -1333,29 +1385,7 @@
     f32 = jnp.float32
     bf16 = jnp.bfloat16
 
-    def halve(n, k):
-        return np.tile((np.arange(n)[:, None] // 2 == np.arange(n // 2)[None, :]).astype(np.float32) * 0.25, (1, k))
-
-    downy = halve(n0, 1)
-    upy = halve(n0, 1).T * 4.0
-    down2 = np.zeros((r1 // 2 * n1, 128), np.float32)
-    up2 = np.zeros((r1 // 2, 128, n1), np.float32)
-    down3 = np.zeros((128, 128), np.float32)
-    up3 = np.zeros((128, 128), np.float32)
-    for i in range(r1 // 2):
-        down2[i * n1 : (i + 1) * n1, i * n2 : (i + 1) * n2] = halve(n1, 1)
-        up2[i, i * n2 : (i + 1) * n2, :] = halve(n1, 1).T * 4.0
-        down3[i * n2 : (i + 1) * n2] = halve(n2, 128 // n3)
-        up3[3 * n3 : 4 * n3, i * n2 : (i + 1) * n2] = halve(n2, 1).T * 4.0
-    down4 = np.zeros((128, 128), np.float32)
-    down4[3 * n3 : 4 * n3] = halve(n3, 128 // n4)
-    up4 = np.zeros((2, 2, 128, 128), np.float32)
-    for par in range(2):
-        for s in range(1, 6):
-            r = 4 + (par - 3 + s) // 2
-            up4[par, s // 4, r * n4 : (r + 1) * n4, s % 4 * n3 : (s % 4 + 1) * n3] = halve(n3, 1).T * 4.0
-    consts = [jnp.asarray(c, bf16) for c in (downy, upy, down2, up2, down3, down4, up3, up4)]
-    vm = pl.BlockSpec(memory_space=pltpu.VMEM)
+    hbm = pl.BlockSpec(memory_space=pl.ANY)
     sm = pl.BlockSpec(memory_space=pltpu.SMEM)
     ns = (zall - 1).bit_length()
     dma = pltpu.SemaphoreType.DMA
@@ -1363,11 +1393,21 @@
         functools.partial(chain_kernel, (gz, gy, depth)),
         out_shape=(
             jax.ShapeDtypeStruct(source.shape, f32),
-            jax.ShapeDtypeStruct((8, 128), f32),
+            jax.ShapeDtypeStruct((CYCLES,), f32),
         ),
-        in_specs=[vm, vm, sm] + [vm] * len(consts),
-        out_specs=(vm, vm),
+        in_specs=[pl.BlockSpec(memory_space=pltpu.HBM)] * 2 + [sm],
+        out_specs=(hbm, sm),
         scratch_shapes=[
+            pltpu.VMEM(source.shape, f32),
+            pltpu.VMEM(source.shape, f32),
+            pltpu.VMEM((n0, n1), bf16),
+            pltpu.VMEM((n1, n0), bf16),
+            pltpu.VMEM((r1 // 2, 128, n1), bf16),
+            pltpu.VMEM((128, 128), bf16),
+            pltpu.VMEM((2, 128, 128), bf16),
+            pltpu.VMEM((2, 128, 128), bf16),
+            pltpu.VMEM((2, 128, 128), bf16),
+            pltpu.SemaphoreType.DMA((3,)),
             pltpu.VMEM((3, r0 + 4, zall + 2 * PAD, n0), f32),
             pltpu.VMEM((r0 + 2, zall, n0), f32),
             pltpu.VMEM((r0 + 2, zall, n0), f32),
@@ -1386,8 +1426,8 @@
             pltpu.VMEM((CYCLES, 3, zall, 128), f32),
             pltpu.VMEM((CYCLES, 3, zall, 128), f32),
             pltpu.VMEM((3, zall, 128), f32),
-            pltpu.VMEM((CYCLES + 1, 7, n3 * zall // 128, 128), f32),
-            pltpu.VMEM((CYCLES + 1, 18, n4 * zall // 128, 128), f32),
+            pltpu.VMEM((CYCLES + 1, 8, n3 * zall // 128, 128), f32),
+            pltpu.VMEM((CYCLES + 1, 9, n4 * zall // 128, 128), f32),
             pltpu.VMEM((2, 5, zall, 128), f32),
             pltpu.VMEM((2, 4, zall, 128), f32),
             pltpu.VMEM((2, 4, zall, 128), f32),
@@ -1399,20 +1439,21 @@
             pltpu.VMEM((CYCLES, 8, 128), f32),
             pltpu.VMEM((8, 128), f32),
             pltpu.VMEM((nd, 8, 128), f32),
-            dma((5, nd)),
-            dma((5, nd)),
-            dma((8 + 2 * CYCLES, 2)),
-            dma((8 + 2 * CYCLES, 2)),
-            dma((CYCLES + 1, 7)),
-            dma((CYCLES + 1, 7)),
-            dma((CYCLES + 1, 18)),
-            dma((CYCLES + 1, 18)),
+            dma((5,)),
+            dma((5,)),
+            dma((nd,)),
+            dma((10, 2)),
+            dma((10, 2)),
+            dma((10,)),
+            dma((2, 8)),
+            dma((9,)),
+            dma((2, 9)),
         ],
         compiler_params=pltpu.CompilerParams(
-            has_side_effects=True, vmem_limit_bytes=64000 * 1024
+            has_side_effects=True, vmem_limit_bytes=VMEM_LIMIT
         ),
-    )(source, reaction, vertical, *consts)
-    return solution, norms[:CYCLES, 0]
+    )(source, reaction, vertical)
+    return solution, norms
 
 
 def shards_of(gz, gy, source, vertical, reaction):

time: 190 us -> 182 us (0.958)
  Pallas kernels: 185 us -> 178 us
    pallas_call x1, Pallas kernels: 185 us -> 178 us  [chain_shards(): pl.pallas_call(functools.partial(chain_kernel, (gz, gy, depth)), out_shap...]
where the time goes in v2:
time: 182 us
  Pallas kernels  178 us (98%)
  local copies, waits for them, and re-layouts  2.8 us (2%)
    pallas_call x1, Pallas kernels, chain_shards(): pl.pallas_call(functools.partial(chain_kernel, (gz, gy, depth)), out_shap...  178 us

profile of v2, /device:TPU:0, one launch (start us, length us, event | category | flops | bytes accessed | tf_op | source)
XLA Modules:
  0.0 181.8 jit_solution(12930613258545246104)
XLA Ops:
  0.6 178.3 %shard_map.50 = (f32[4,256,256]{2,1,0:T(8,128)}, f32[2]{0:T(128)}) custom-call(f32[4,256,256]{2,1,0:T(8,128)} %source_in.1, f32[4,256,256]{2,1,0:T(8,128)} %reaction_in.1, f32[4]{0:T(128)} %vertical.1), custom_call_target="tpu_custom_call" | custom-call | tf_op jit(solution)/shard_map/pallas_call | solution.py:1392
  179.0 0.0 copy-start
  179.0 2.3 %copy.7 = f32[4,256,256]{2,1,0:T(8,128)} copy(f32[4,256,256]{2,1,0:T(8,128)} %get-tuple-element.4) | data formatting | bytes 2097152
  181.3 0.0 copy-done
  181.3 0.5 copy.8
Async XLA Ops:
  179.0 2.3 %copy-start = (f32[2]{0:T(128)S(1)}, f32[2]{0:T(128)}, u32[]{:S(2)}) copy-start(f32[2]{0:T(128)} %get-tuple-element.5) | copy-start | bytes 28

commit v3 on v2

--- a/solution.py
+++ b/solution.py
@@ -586,6 +586,7 @@
 
 
 CROWS = 32
+GROUP = 2
 VMEM_LIMIT = 64000 * 1024
 PAD = 8
 
@@ -624,13 +625,19 @@
     me = a_me * gy + b_me
     nchip = gz // 2
 
+    def div(x, n):
+        return lax.div(x, jnp.int32(n))
+
+    def rem(x, n):
+        return lax.rem(x, jnp.int32(n))
+
     def bend(c):
-        return c + c // 2 - 2 * (c // 3) if nchip == 4 else c
+        return c + div(c, 2) - 2 * div(c, 3) if nchip == 4 else c
 
     def place(i):
-        k, core = i // 2, i % 2
-        b, q = k // nchip, k % nchip
-        q = q + (b % 2) * (nchip - 1 - 2 * q)
+        k, core = div(i, 2), rem(i, 2)
+        b, q = div(k, nchip), rem(k, nchip)
+        q = q + rem(b, 2) * (nchip - 1 - 2 * q)
         return (bend(q) * 2 + core, b)
 
     q_me = bend(a_me // 2)
@@ -650,7 +657,7 @@
         )
 
     def target(k):
-        return (p + nd + (k // 2 + k % 2) * (1 - 2 * (k % 2))) % nd
+        return rem(p + nd + (div(k, 2) + rem(k, 2)) * (1 - 2 * rem(k, 2)), nd)
 
     def flat(i):
         a, b = place(i)
@@ -673,7 +680,7 @@
                 r = each(s)
                 remote(r, r, a2a_send.at[kind], from_sem.at[s], place(p)).wait_recv()
 
-        return lambda: loop(1, nd, start), lambda: wait_all(False), landed
+        return lambda lo=1, hi=nd: loop(lo, hi, start), lambda: wait_all(False), landed
 
     def piece(ref, t):
         return ref.at[:, pl.ds(r0 * t, r0), :]
@@ -757,6 +764,9 @@
         def at(lo):
             return v0.at[m, pl.ds(lo, dep), pl.ds(PAD, zall), :]
         return xchg(m, at(2), at(2 - dep), at(2 + r0 - dep), at(2 + r0))
+
+    def row1(kind, far):
+        return xchg(kind, g1.at[2 + far], g1.at[1 - far], g1.at[r1 + 1 - far], g1.at[r1 + 2 + far])
 
     def planes1(ref, kind):
         return xchg(kind, ref.at[pl.ds(2, 2)], ref.at[pl.ds(0, 2)],
@@ -891,8 +901,6 @@
             def _(o=o, k=k):
                 win4[k, 4 + o] = jnp.zeros((n4 * zall // 128, 128), f32)
     for q in range(2):
-        v2[q, 0] = tile0
-        v2[q, 4] = tile0
         v3[q, 0] = tile0
         v3[q, 3] = tile0
         v4[q, 0] = tile0
@@ -1104,21 +1112,25 @@
 
     def sweep_plane(level, m, q, x, record=None, put=None):
         v, g, w, d, nt, weight, go = level
-        for r in range(0, zall, CROWS):
-            centre, got = stencil(level, m, x, r)
-            for t in range(nt):
-                cut = slice(128 * t, 128 * (t + 1))
-                wt = w[x + go, r : r + CROWS, cut]
-                if record is None:
-                    new = (1.0 - DAMPING) * centre[t] + wt * got[t]
-                else:
-                    res = got[t] - d[x + go, r : r + CROWS, cut] * centre[t]
-                    new = centre[t] + wt * res
-                    acc[record] += (res * res).reshape(CROWS // 8, 8, 128).sum(axis=0)
-                v[q, x + 2, PAD + r : PAD + r + CROWS, cut] = new
+        for lo in range(0, zall, GROUP * CROWS):
+            new = []
+            for r in range(lo, lo + GROUP * CROWS, CROWS):
+                centre, got = stencil(level, m, x, r)
+                for t in range(nt):
+                    cut = slice(128 * t, 128 * (t + 1))
+                    wt = w[x + go, r : r + CROWS, cut]
+                    if record is None:
+                        value = (1.0 - DAMPING) * centre[t] + wt * got[t]
+                    else:
+                        res = got[t] - d[x + go, r : r + CROWS, cut] * centre[t]
+                        value = centre[t] + wt * res
+                        acc[record] += (res * res).reshape(CROWS // 8, 8, 128).sum(axis=0)
+                    new.append((r, t, value))
+            for r, t, value in new:
+                v[q, x + 2, PAD + r : PAD + r + CROWS, 128 * t : 128 * (t + 1)] = value
                 if put is not None:
                     for e in range(0, CROWS, 8):
-                        put(x, r + e, t, new[e : e + 8])
+                        put(x, r + e, t, value[e : e + 8])
 
     def residual(level, m, x, r):
         v, g, w, d, nt, weight, go = level
@@ -1160,6 +1172,7 @@
         sweeps(level0, m, 1, (1, r0 - 1, same), record)
         if restrict:
             restrict0(1, 1, r1 - 1, same)
+            row1(3, 1)[0]()
         else:
             sweeps(level0, 1, q, (2, r0 - 2, same), None, put)
         end()
@@ -1177,6 +1190,8 @@
         for t in range(3):
             diag[t] = 2.0 * lines[...] + 4.0 * h[2] + dx[t]
         loop(0, 3, factors)
+        for k in range(2 * ns + 1):
+            fac[7, k] = jnp.where(lane >= n2, fac[0, k], fac[2, k])
         end_w3()
         unpack3(CYCLES, g3)
         win4[CYCLES, 4] = pack(
@@ -1210,11 +1225,12 @@
                     w1[x + q] = DAMPING / d1[x + q]
 
     def coarse(cycle):
-        begin, end = planes1(g1, 3)
+        begin, end = row1(10, 0)
         begin()
         if cycle == 0:
             window_factors()
         loop(2, r1 + 2, lambda x: v1.__setitem__((0, x, pl.ds(PAD, zall)), w1[x] * g1[x]))
+        row1(3, 1)[1]()
         end()
         if cycle == 0:
             halo_level1()
@@ -1246,8 +1262,8 @@
         sweeps(level1, 1, 0, (0, r1, same))
 
     def lines_sweep(v, q, s, lo, hi, right, f, weight, width):
-        loop(lo, hi, lambda b: v.__setitem__(
-            (s, b), solve(f + b - 1, right[b - 1] + weight * near(v, q, b, width))))
+        for b in range(lo, hi):
+            v[s, b] = solve(f + b - 1, right[b - 1] + weight * near(v, q, b, width))
 
     def line_residual(v, q, b, right, f, weight, width):
         values = v[q, b]
@@ -1255,25 +1271,40 @@
         after = jnp.where(rows == zall - 1, 0.0, pltpu.roll(values, zall - 1, 0))
         return right[b - 1] + weight * near(v, q, b, width) + lines[...] * (before + after) - diag[f + b - 1] * values
 
+    def beside(t):
+        inrow = lane % n2
+        return jnp.where(inrow == 0, 0.0, pltpu.roll(t, 1, 1)) + jnp.where(inrow == n2 - 1, 0.0, pltpu.roll(t, 127, 1))
+
+    def pair2(left, own, right, right_own, right_rim):
+        upper = lane >= n2
+        rim = jnp.where(upper, left, right)
+        far = jnp.where(upper, right, left)
+        new = solve(1, right_own + h[2] * (beside(own) + pltpu.roll(own + rim, n2, 1)))
+        return new, solve(7, right_rim + h[2] * (beside(rim) + pltpu.roll(own + far, n2, 1)))
+
     def lines2(cycle):
         right = gx.at[cycle]
         begin, end = blocks(right, 8)
         begin()
-        v2[0, 2] = solve(1, right[1])
+        v2[1] = solve(1, right[1])
         end()
-        loop(0, 2, lambda i: v2.__setitem__((0, 1 + 2 * i), solve(2 * i, right[2 * i])))
-        lines_sweep(v2, 0, 1, 1, 4, right, 0, h[2], n2)
-        res = line_residual(v2, 1, 2, right, 0, h[2], n2)
+        for b in (0, 2):
+            v2[b] = solve(b, right[b])
+        right_rim = jnp.where(lane >= n2, right[0], right[2])
+        v2[3], v2[4] = pair2(v2[0], v2[1], v2[2], right[1], right_rim)
+        own = v2[3]
+        before = jnp.where(rows == 0, 0.0, pltpu.roll(own, 1, 0))
+        after = jnp.where(rows == zall - 1, 0.0, pltpu.roll(own, zall - 1, 0))
+        around = beside(own) + pltpu.roll(own + v2[4], n2, 1)
+        res = right[1] + h[2] * around + lines[...] * (before + after) - diag[1] * own
         win3[cycle, 3 + par] = pack(dot_parts(res, down3[...]), n3)
         e3 = lines3(cycle)
-        cx[cycle, 1] = v2[1, 2] + dot_parts(e3, up3[par])
+        cx[cycle, 1] = v2[3] + dot_parts(e3, up3[par])
         begin, end = blocks(cx.at[cycle], 9)
         begin()
         end()
-        for b in range(3):
-            v2[0, b + 1] = cx[cycle, b]
-        lines_sweep(v2, 0, 1, 1, 4, right, 0, h[2], n2)
-        return solve(1, right[1] + h[2] * near(v2, 1, 2, n2))
+        v2[0], v2[1] = pair2(cx[cycle, 0], cx[cycle, 1], cx[cycle, 2], right[1], jnp.where(lane >= n2, right[0], right[2]))
+        return solve(1, right[1] + h[2] * (beside(v2[0]) + pltpu.roll(v2[0] + v2[1], n2, 1)))
 
     def lines3(cycle):
         begin, end = window3(cycle)
@@ -1330,6 +1361,7 @@
     begin, end = planes0(2, 1)
     begin()
     restrict0(2, 1, r1 - 1, same)
+    row1(3, 1)[0]()
     end()
     restrict0(2, 0, 2, lambda i: i * (r1 - 1))
     coarse(1)
@@ -1338,7 +1370,7 @@
     loop(0, zall // PAD, fold)
     begin, end = planes0(2, 1)
     begin()
-    start_o()
+    start_o(1, nd * 5 // 8)
     keep = pltpu.make_async_copy(zrows(stage, me), piece(out, p), load.at[2])
     keep.start()
 
@@ -1356,6 +1388,7 @@
         part = jnp.where(ridx == k, jnp.sum(acc[k]), part)
     nsend[...] = part
     start_n()
+    start_o(nd * 5 // 8, nd)
     total = part
     done_v()
     done_r()
@@ -1385,18 +1418,17 @@
     f32 = jnp.float32
     bf16 = jnp.bfloat16
 
-    hbm = pl.BlockSpec(memory_space=pl.ANY)
     sm = pl.BlockSpec(memory_space=pltpu.SMEM)
     ns = (zall - 1).bit_length()
     dma = pltpu.SemaphoreType.DMA
     solution, norms = pl.pallas_call(
         functools.partial(chain_kernel, (gz, gy, depth)),
         out_shape=(
-            jax.ShapeDtypeStruct(source.shape, f32),
+            pltpu.VMEM(source.shape, f32),
             jax.ShapeDtypeStruct((CYCLES,), f32),
         ),
         in_specs=[pl.BlockSpec(memory_space=pltpu.HBM)] * 2 + [sm],
-        out_specs=(hbm, sm),
+        out_specs=(pl.BlockSpec(memory_space=pltpu.VMEM), sm),
         scratch_shapes=[
             pltpu.VMEM(source.shape, f32),
             pltpu.VMEM(source.shape, f32),
@@ -1428,13 +1460,13 @@
             pltpu.VMEM((3, zall, 128), f32),
             pltpu.VMEM((CYCLES + 1, 8, n3 * zall // 128, 128), f32),
             pltpu.VMEM((CYCLES + 1, 9, n4 * zall // 128, 128), f32),
-            pltpu.VMEM((2, 5, zall, 128), f32),
+            pltpu.VMEM((5, zall, 128), f32),
             pltpu.VMEM((2, 4, zall, 128), f32),
             pltpu.VMEM((2, 4, zall, 128), f32),
             pltpu.VMEM((2, zall, 128), f32),
             pltpu.VMEM((2, zall, 128), f32),
             pltpu.VMEM((7, zall, 128), f32),
-            pltpu.VMEM((7, 2 * ns + 1, zall, 128), f32),
+            pltpu.VMEM((8, 2 * ns + 1, zall, 128), f32),
             pltpu.VMEM((7, zall, 128), f32),
             pltpu.VMEM((CYCLES, 8, 128), f32),
             pltpu.VMEM((8, 128), f32),
@@ -1442,8 +1474,8 @@
             dma((5,)),
             dma((5,)),
             dma((nd,)),
-            dma((10, 2)),
-            dma((10, 2)),
+            dma((11, 2)),
+            dma((11, 2)),
             dma((10,)),
             dma((2, 8)),
             dma((9,)),

time: 182 us -> 177 us (0.973); the launches traced: 182 us -> 175 us
  Pallas kernels: 178 us -> 173 us
    pallas_call x1, Pallas kernels: 178 us -> 173 us  [chain_shards(): pl.pallas_call(functools.partial(chain_kernel, (gz, gy, depth)), out_shap...]
where the time goes in v3:
time: 177 us; the launch traced here: 175 us
  Pallas kernels  173 us (98%)
    pallas_call x1, Pallas kernels, chain_shards(): pl.pallas_call(functools.partial(chain_kernel, (gz, gy, depth)), out_shap...  173 us

profile of v3, /device:TPU:0, one launch (start us, length us, event | category | flops | bytes accessed | tf_op | source)
XLA Modules:
  0.0 174.8 jit_solution(5009990993467784162)
XLA Ops:
  0.6 172.7 %shard_map.50 = (f32[4,256,256]{2,1,0:T(8,128)S(1)}, f32[2]{0:T(128)}) custom-call(f32[4,256,256]{2,1,0:T(8,128)} %source_in.1, f32[4,256,256]{2,1,0:T(8,128)} %reaction_in.1, f32[4]{0:T(128)} %vertical.1), custom_call_target="tpu_custom_call" | custom-call | tf_op jit(solution)/shard_map/pallas_call | solution.py:1424
  173.3 0.0 copy-start
  173.3 1.0 copy.7
  174.3 0.0 copy-done
  174.3 0.5 copy.8
Async XLA Ops:
  173.3 1.0 copy-start

commit v4 on v3

--- a/solution.py
+++ b/solution.py
@@ -609,7 +609,7 @@
     out, norms,
     source, reaction, downy, upy, up2, down3, down4, up3, up4, load,
     v0, g0, w0, d0, v1, g1, w1, d1, raw_r, raw_s, stage, turn, lines, vsend, vrecv,
-    gx, cx, dx, win3, win4, v2, v3, v4, g3, g4, diag, fac, mask, acc, nsend, nrecv,
+    gx, cx, ex, dx, win3, win4, v2, v3, v4, g3, g4, diag, fac, mask, acc, nsend, nrecv,
     a2a_send, a2a_recv, from_sem, x_send, x_recv, w3_send, w3_recv, w4_send, w4_recv,
 ):
     gz, gy, depth = dims
@@ -738,14 +738,16 @@
         def up():
             return remote(hi_src, lo_dst, x_send.at[kind, 1], x_recv.at[kind, 1], place((p + 1) % nd))
 
-        def begin():
-            @pl.when(jnp.logical_not(first))
-            def _():
-                down().start()
-
-            @pl.when(jnp.logical_not(last))
-            def _():
-                up().start()
+        def begin(sides=(0, 1)):
+            if 0 in sides:
+                @pl.when(jnp.logical_not(first))
+                def _():
+                    down().start()
+
+            if 1 in sides:
+                @pl.when(jnp.logical_not(last))
+                def _():
+                    up().start()
 
         def end():
             @pl.when(jnp.logical_not(first))
@@ -772,10 +774,25 @@
         return xchg(kind, ref.at[pl.ds(2, 2)], ref.at[pl.ds(0, 2)],
                     ref.at[pl.ds(r1, 2)], ref.at[pl.ds(r1 + 2, 2)])
 
-    def planes1v(m):
-        def at(lo):
-            return v1.at[m, pl.ds(lo, 2), pl.ds(PAD, zall), :]
-        return xchg(4, at(2), at(0), at(r1), at(r1 + 2))
+    def far0(m):
+        def at(x):
+            return v0.at[m, x, pl.ds(PAD, zall), :]
+        return xchg(11, at(3), at(0), at(r0), at(r0 + 3))
+
+    def norm0():
+        def at(m, x):
+            return v0.at[m, x, pl.ds(PAD, zall), :]
+        return xchg(1, at(2, 2), at(1, 0), at(2, r0 + 1), at(1, r0 + 3))
+
+    def rows1():
+        def at(x):
+            return v1.at[0, x, pl.ds(PAD, zall), :]
+        return xchg(12, at(2), at(1), at(r1 + 1), at(r1 + 2))
+
+    def far1():
+        def at(x):
+            return v1.at[1, x, pl.ds(PAD, zall), :]
+        return xchg(13, at(3), at(0), at(r1), at(r1 + 3))
 
     def blocks(ref, kind):
         return xchg(kind, ref.at[1], ref.at[0], ref.at[1], ref.at[2])
@@ -870,9 +887,9 @@
 
     def blank(lo0, x0, lo1, b):
         for q in range(2):
-            for m in (0, 2):
+            for m in range(3):
                 v0[m, lo0 + q, PAD : PAD + zall, :] = plane0
-            v1[2, lo1 + q, PAD : PAD + zall, :] = tile0
+            v1[1, lo1 + q, PAD : PAD + zall, :] = tile0
             g1[lo1 + q] = tile0
             d1[lo1 + q] = tile0
             w1[lo1 + q] = tile0
@@ -881,6 +898,7 @@
         for k in range(CYCLES):
             gx[k, b] = tile0
             cx[k, b] = tile0
+            ex[k, b] = tile0
         dx[b] = tile0
 
     @pl.when(first)
@@ -1156,17 +1174,13 @@
     def same(i):
         return i
 
-    def rim(size, wide):
-        return lambda i: i + (i // wide) * (size - 2 * wide)
-
-    def outer(size):
-        return lambda i: -1 + i * (size + 1)
-
-    def pair0(m, q, record=None, hook=None, put=None, restrict=False, before=None):
-        begin, end = planes0(m, 2)
-        begin()
-        if before is not None:
-            before()
+    def pair0(m, q, then, record=None, hook=None, put=None, restrict=False, fix=None):
+        if fix is None:
+            end = planes0(m, 2)[1]
+        else:
+            end = rows1()[1]
+            far0(fix)[1]()
+            correct0(fix, m, 0, r1, same)
         if hook is not None:
             hook[0]()
         sweeps(level0, m, 1, (1, r0 - 1, same), record)
@@ -1178,12 +1192,17 @@
         end()
         if hook is not None:
             hook[1]()
-        sweeps(level0, m, 1, (0, 2, outer(r0)))
-        sweeps(level0, m, 1, (0, 2, rim(r0, 1)), record)
-        if restrict:
-            restrict0(1, 0, 2, lambda i: i * (r1 - 1))
-        else:
-            sweeps(level0, 1, q, (0, 4, rim(r0, 2)), None, put)
+        for side in range(2):
+            if fix is not None:
+                correct0(fix, m, 0, 1, lambda i: r1 if side else -1)
+            sweep_plane(level0, m, 1, r0 if side else -1)
+            sweep_plane(level0, m, 1, r0 - 1 if side else 0, record)
+            if restrict:
+                restrict0(1, 0, 1, lambda i: r1 - 1 if side else 0)
+            else:
+                for k in range(2):
+                    sweep_plane(level0, 1, q, r0 - 2 + k if side else k, None, put)
+            then((side,))
 
     def halo_factors():
         end_dx()
@@ -1224,9 +1243,9 @@
                 for q in range(2):
                     w1[x + q] = DAMPING / d1[x + q]
 
-    def coarse(cycle):
-        begin, end = row1(10, 0)
-        begin()
+    def coarse(cycle, m):
+        end = row1(10, 0)[1]
+        far0(m)[0]()
         if cycle == 0:
             window_factors()
         loop(2, r1 + 2, lambda x: v1.__setitem__((0, x, pl.ds(PAD, zall)), w1[x] * g1[x]))
@@ -1247,19 +1266,28 @@
                 cuts.append(a + b)
             pairs.append(jnp.concatenate(cuts, axis=0))
         gx[cycle, 1] = dot_parts(jnp.concatenate(pairs, axis=1), downy[...])
-        e2 = lines2(cycle)
+        e2 = lines2(cycle, far1()[0])
+        ex[cycle, 1] = e2
+        begin, end = blocks(ex.at[cycle], 4)
+        begin()
 
         for i in range(r1 // 2):
             e = dot_parts(e2, up2[i])
             for x in (2 * i, 2 * i + 1):
                 v1[2, x + 2, PAD : PAD + zall] = v1[1, x + 2, PAD : PAD + zall] + e
-        begin, end = planes1v(2)
-        begin()
+        far1()[1]()
         sweeps(level1, 2, 1, (1, r1 - 1, same))
         end()
-        sweeps(level1, 2, 1, (0, 2, outer(r1)))
-        sweeps(level1, 2, 1, (0, 2, rim(r1, 1)))
-        sweeps(level1, 1, 0, (0, r1, same))
+        for side in range(2):
+            e = dot_parts(ex[cycle, 2], up2[0]) if side else dot_parts(ex[cycle, 0], up2[r1 // 2 - 1])
+            for x in (r1 + 2, r1 + 3) if side else (0, 1):
+                v1[2, x, PAD : PAD + zall] = v1[1, x, PAD : PAD + zall] + e
+        for x in (-1, 0, r1 - 1, r1):
+            sweep_plane(level1, 2, 1, x)
+        for x in (0, r1 - 1):
+            sweep_plane(level1, 1, 0, x)
+        rows1()[0]()
+        sweeps(level1, 1, 0, (1, r1 - 1, same))
 
     def lines_sweep(v, q, s, lo, hi, right, f, weight, width):
         for b in range(lo, hi):
@@ -1282,10 +1310,11 @@
         new = solve(1, right_own + h[2] * (beside(own) + pltpu.roll(own + rim, n2, 1)))
         return new, solve(7, right_rim + h[2] * (beside(rim) + pltpu.roll(own + far, n2, 1)))
 
-    def lines2(cycle):
+    def lines2(cycle, after):
         right = gx.at[cycle]
         begin, end = blocks(right, 8)
         begin()
+        after()
         v2[1] = solve(1, right[1])
         end()
         for b in (0, 2):
@@ -1353,23 +1382,22 @@
         for t in range(nt0):
             staged[at, 128 * t : 128 * (t + 1)] = turn[t, at, :]
 
-    pair0(0, 1, hook=(halo_factors, halo_level0), restrict=True)
-    coarse(0)
-    correct0(1, 2, 0, 2, lambda i: i * (r1 - 1))
-    pair0(2, 0, before=lambda: correct0(1, 2, 1, r1 - 1, same))
-    pair0(0, 2, record=0)
-    begin, end = planes0(2, 1)
-    begin()
+    planes0(0, 2)[0]()
+    pair0(0, 1, row1(10, 0)[0], hook=(halo_factors, halo_level0), restrict=True)
+    coarse(0, 1)
+    pair0(2, 0, planes0(0, 2)[0], fix=1)
+    pair0(0, 2, planes0(2, 1)[0], record=0)
+    end = planes0(2, 1)[1]
     restrict0(2, 1, r1 - 1, same)
     row1(3, 1)[0]()
     end()
-    restrict0(2, 0, 2, lambda i: i * (r1 - 1))
-    coarse(1)
-    correct0(2, 0, 0, 2, lambda i: i * (r1 - 1))
-    pair0(0, 2, put=put, before=lambda: correct0(2, 0, 1, r1 - 1, same))
+    for side in range(2):
+        restrict0(2, 0, 1, lambda i: r1 - 1 if side else 0)
+        row1(10, 0)[0]((side,))
+    coarse(1, 2)
+    pair0(0, 2, norm0()[0], put=put, fix=2)
     loop(0, zall // PAD, fold)
-    begin, end = planes0(2, 1)
-    begin()
+    end = norm0()[1]
     start_o(1, nd * 5 // 8)
     keep = pltpu.make_async_copy(zrows(stage, me), piece(out, p), load.at[2])
     keep.start()
@@ -1381,6 +1409,8 @@
 
     loop(1, r0 - 1, last_norm)
     end()
+    for x, y in ((1, 0), (r0 + 2, r0 + 3)):
+        v0[2, x, PAD : PAD + zall, :] = v0[1, y, PAD : PAD + zall, :]
     loop(0, 2, lambda i: last_norm(i * (r0 - 1)))
     ridx = lax.broadcasted_iota(jnp.int32, (8, 128), 0)
     part = jnp.zeros((8, 128), f32)
@@ -1457,6 +1487,7 @@
             pltpu.VMEM((nd, depth, 128), f32),
             pltpu.VMEM((CYCLES, 3, zall, 128), f32),
             pltpu.VMEM((CYCLES, 3, zall, 128), f32),
+            pltpu.VMEM((CYCLES, 3, zall, 128), f32),
             pltpu.VMEM((3, zall, 128), f32),
             pltpu.VMEM((CYCLES + 1, 8, n3 * zall // 128, 128), f32),
             pltpu.VMEM((CYCLES + 1, 9, n4 * zall // 128, 128), f32),
@@ -1474,8 +1505,8 @@
             dma((5,)),
             dma((5,)),
             dma((nd,)),
-            dma((11, 2)),
-            dma((11, 2)),
+            dma((14, 2)),
+            dma((14, 2)),
             dma((10,)),
             dma((2, 8)),
             dma((9,)),

time: 177 us -> 167 us (0.944)
  Pallas kernels: 173 us -> 164 us
    pallas_call x1, Pallas kernels: 173 us -> 164 us  [chain_shards(): pl.pallas_call(functools.partial(chain_kernel, (gz, gy, depth)), out_shap...]
where the time goes in v4:
time: 167 us; the launch traced here: 166 us
  Pallas kernels  164 us (98%)
    pallas_call x1, Pallas kernels, chain_shards(): pl.pallas_call(functools.partial(chain_kernel, (gz, gy, depth)), out_shap...  164 us

profile of v4, /device:TPU:0, one launch (start us, length us, event | category | flops | bytes accessed | tf_op | source)
XLA Modules:
  0.0 166.5 jit_solution(14067558446941952146)
XLA Ops:
  0.6 164.4 %shard_map.50 = (f32[4,256,256]{2,1,0:T(8,128)S(1)}, f32[2]{0:T(128)}) custom-call(f32[4,256,256]{2,1,0:T(8,128)} %source_in.1, f32[4,256,256]{2,1,0:T(8,128)} %reaction_in.1, f32[4]{0:T(128)} %vertical.1), custom_call_target="tpu_custom_call" | custom-call | tf_op jit(solution)/shard_map/pallas_call | solution.py:1454
  165.0 0.0 copy-start
  165.0 1.0 copy.7
  166.0 0.0 copy-done
  166.0 0.5 copy.8
Async XLA Ops:
  165.0 1.0 copy-start

commit v5 on v4

--- a/solution.py
+++ b/solution.py
@@ -702,8 +702,15 @@
     load_s = pltpu.make_async_copy(source_in, source, load.at[1])
     load_r.start()
     load_s.start()
+    barrier = pltpu.get_barrier_semaphore()
+
+    def greet(k):
+        pl.semaphore_signal(barrier, inc=1, device_id=place(target(nd - k)), device_id_type=MESH)
+
+    loop(1, nd, greet)
     for i in range(depth):
         vsend[i : i + 1, :] = jnp.full((1, 128), vertical[i], f32)
+    pl.semaphore_wait(barrier, nd - 1)
     load_r.wait()
     start_r()
     start_v()
@@ -1255,7 +1262,8 @@
             halo_level1()
         for x in (0, 1, r1 + 2, r1 + 3):
             v1[0, x, PAD : PAD + zall] = w1[x] * g1[x]
-        sweeps(level1, 0, 1, (-1, r1 + 1, same))
+        for x in range(-1, r1 + 1):
+            sweep_plane(level1, 0, 1, x)
 
         pairs = []
         for i in range(r1 // 2):
@@ -1276,18 +1284,19 @@
             for x in (2 * i, 2 * i + 1):
                 v1[2, x + 2, PAD : PAD + zall] = v1[1, x + 2, PAD : PAD + zall] + e
         far1()[1]()
-        sweeps(level1, 2, 1, (1, r1 - 1, same))
+        for x in range(1, r1 - 1):
+            sweep_plane(level1, 2, 1, x)
         end()
         for side in range(2):
             e = dot_parts(ex[cycle, 2], up2[0]) if side else dot_parts(ex[cycle, 0], up2[r1 // 2 - 1])
             for x in (r1 + 2, r1 + 3) if side else (0, 1):
                 v1[2, x, PAD : PAD + zall] = v1[1, x, PAD : PAD + zall] + e
-        for x in (-1, 0, r1 - 1, r1):
-            sweep_plane(level1, 2, 1, x)
-        for x in (0, r1 - 1):
+            for x in (r1 - 1, r1) if side else (-1, 0):
+                sweep_plane(level1, 2, 1, x)
+            sweep_plane(level1, 1, 0, r1 - 1 if side else 0)
+            rows1()[0]((side,))
+        for x in range(1, r1 - 1):
             sweep_plane(level1, 1, 0, x)
-        rows1()[0]()
-        sweeps(level1, 1, 0, (1, r1 - 1, same))
 
     def lines_sweep(v, q, s, lo, hi, right, f, weight, width):
         for b in range(lo, hi):
@@ -1368,10 +1377,11 @@
     def correct0(m, q, lo, hi, fn):
         def body(i):
             i = fn(i)
-            for r in range(0, zall, CROWS):
-                e = dot_parts(v1[0, i + 2, PAD + r : PAD + r + CROWS, :], upy[...])
+            for r in range(0, zall, 2 * CROWS):
+                cut = slice(PAD + r, PAD + r + 2 * CROWS)
+                e = dot_parts(v1[0, i + 2, cut, :], upy[...])
                 for x in (2 * i + 2, 2 * i + 3):
-                    v0[q, x, PAD + r : PAD + r + CROWS, :] = v0[m, x, PAD + r : PAD + r + CROWS, :] + e
+                    v0[q, x, cut, :] = v0[m, x, cut, :] + e
         loop(lo, hi, body)
 
     def put(x, z, t, value):
@@ -1513,7 +1523,7 @@
             dma((2, 9)),
         ],
         compiler_params=pltpu.CompilerParams(
-            has_side_effects=True, vmem_limit_bytes=VMEM_LIMIT
+            has_side_effects=True, vmem_limit_bytes=VMEM_LIMIT, collective_id=0
         ),
     )(source, reaction, vertical)
     return solution, norms

time: 167 us -> 161 us (0.964)
  Pallas kernels: 164 us -> 159 us
    pallas_call x1, Pallas kernels: 164 us -> 159 us  [chain_shards(): pl.pallas_call(functools.partial(chain_kernel, (gz, gy, depth)), out_shap...]
where the time goes in v5:
time: 161 us
  Pallas kernels  159 us (99%)
    pallas_call x1, Pallas kernels, chain_shards(): pl.pallas_call(functools.partial(chain_kernel, (gz, gy, depth)), out_shap...  159 us

profile of v5, /device:TPU:0, one launch (start us, length us, event | category | flops | bytes accessed | tf_op | source)
XLA Modules:
  0.0 160.6 jit_solution(4619715491313757448)
XLA Ops:
  0.6 158.5 %shard_map.50 = (f32[4,256,256]{2,1,0:T(8,128)S(1)}, f32[2]{0:T(128)}) custom-call(f32[4,256,256]{2,1,0:T(8,128)} %source_in.1, f32[4,256,256]{2,1,0:T(8,128)} %reaction_in.1, f32[4]{0:T(128)} %vertical.1), custom_call_target="tpu_custom_call" | custom-call | tf_op jit(solution)/shard_map/pallas_call | solution.py:1464
  159.1 0.0 copy-start
  159.2 1.0 copy.7
  160.1 0.0 copy-done
  160.1 0.5 copy.8
Async XLA Ops:
  159.1 1.0 copy-start

commit v6 on v5

--- a/solution.py
+++ b/solution.py
@@ -807,7 +807,7 @@
     def halo_d0():
         return xchg(5, d0.at[1], d0.at[0], d0.at[r0], d0.at[r0 + 1])
 
-    offs3 = [(o, c) for o in (0, -1, 1, -2, 2) for c in range(2)]
+    offs3 = [(o, c) for o in (-2, 2, -1, 1, 0) for c in range(2)]
 
     def window3(kind):
         buf = win3.at[kind]
@@ -850,7 +850,7 @@
 
         return begin, end
 
-    offs4 = [-1, 1, -2, 2, -3, 3, -4, 4]
+    offs4 = [-4, 4, -3, 3, -2, 2, -1, 1]
 
     def window4(kind):
         buf = win4.at[kind]
@@ -1349,7 +1349,8 @@
         begin()
         end()
         unpack3(cycle, g3)
-        loop(1, 3, lambda b: v3.__setitem__((0, b), solve(3 + b - 1, g3[b - 1])))
+        for b in range(1, 3):
+            v3[0, b] = solve(3 + b - 1, g3[b - 1])
         lines_sweep(v3, 0, 1, 1, 3, g3, 3, h[3], n3)
         both = None
         for t in range(2):
@@ -1367,7 +1368,8 @@
         begin()
         end()
         unpack4(cycle, g4)
-        loop(1, 3, lambda b: v4.__setitem__((0, b), solve(5 + b - 1, g4[b - 1])))
+        for b in range(1, 3):
+            v4[0, b] = solve(5 + b - 1, g4[b - 1])
         q = 0
         for k in range(1, COARSE - 1):
             v4[1 - q, 1] = solve(5, g4[0] + h[4] * near(v4, q, 1, n4))
@@ -1408,7 +1410,7 @@
     pair0(0, 2, norm0()[0], put=put, fix=2)
     loop(0, zall // PAD, fold)
     end = norm0()[1]
-    start_o(1, nd * 5 // 8)
+    start_o(1, nd * 7 // 8)
     keep = pltpu.make_async_copy(zrows(stage, me), piece(out, p), load.at[2])
     keep.start()
 
@@ -1428,7 +1430,7 @@
         part = jnp.where(ridx == k, jnp.sum(acc[k]), part)
     nsend[...] = part
     start_n()
-    start_o(nd * 5 // 8, nd)
+    start_o(nd * 7 // 8, nd)
     total = part
     done_v()
     done_r()
@@ -1465,7 +1467,7 @@
         functools.partial(chain_kernel, (gz, gy, depth)),
         out_shape=(
             pltpu.VMEM(source.shape, f32),
-            jax.ShapeDtypeStruct((CYCLES,), f32),
+            pltpu.SMEM((CYCLES,), f32),
         ),
         in_specs=[pl.BlockSpec(memory_space=pltpu.HBM)] * 2 + [sm],
         out_specs=(pl.BlockSpec(memory_space=pltpu.VMEM), sm),

time: 161 us -> 159 us (0.988)
  Pallas kernels: 159 us -> 157 us
where the time goes in v6:
time: 159 us
  Pallas kernels  157 us (99%)
    pallas_call x1, Pallas kernels, chain_shards(): pl.pallas_call(functools.partial(chain_kernel, (gz, gy, depth)), out_shap...  157 us

profile of v6, /device:TPU:0, one launch (start us, length us, event | category | flops | bytes accessed | tf_op | source)
XLA Modules:
  0.0 159.3 jit_solution(13465204012042634798)
XLA Ops:
  0.6 157.0 %shard_map.50 = (f32[4,256,256]{2,1,0:T(8,128)S(1)}, f32[2]{0:T(128)S(4)}) custom-call(f32[4,256,256]{2,1,0:T(8,128)} %source_in.1, f32[4,256,256]{2,1,0:T(8,128)} %reaction_in.1, f32[4]{0:T(128)} %vertical.1), custom_call_target="tpu_custom_call" | custom-call | tf_op jit(solution)/shard_map/pallas_call | solution.py:1466
  157.6 1.0 copy.7
  158.6 0.5 copy.8
